TPU v7x, 16 devices: a whole 2x2x2 slice. The times are simulated.
16 devices in a mesh: replica: 2 (over z), data: 8 (over y, x, core).
Axes of the slice: x: 2, y: 2, z: 2, core: 2. Of those that a mesh axis runs over, the one named last changes fastest.
Arguments:
- inp_rows: bfloat16 [65536, 896], P(('replica', 'data'))
- out_grad: bfloat16 [65536, 896], P(('replica', 'data'))
- w_up: bfloat16 [2, 896, 4864], replicated
- w_down: bfloat16 [2, 4864, 896], replicated
- master_up: float32 [2, 896, 4864], P(None, 'data')
- master_down: float32 [2, 4864, 896], P(None, 'data')
- mom_up: float32 [2, 896, 4864], P(None, 'data')
- mom_down: float32 [2, 4864, 896], P(None, 'data')
- var_up: float32 [2, 896, 4864], P(None, 'data')
- var_down: float32 [2, 4864, 896], P(None, 'data')
- clip_norm: float32 [], replicated
Outputs:
- output 1: bfloat16 [2, 896, 4864], replicated
- output 2: bfloat16 [2, 4864, 896], replicated
- output 3: float32 [2, 896, 4864], P(None, 'data')
- output 4: float32 [2, 4864, 896], P(None, 'data')
- output 5: float32 [2, 896, 4864], P(None, 'data')
- output 6: float32 [2, 4864, 896], P(None, 'data')
- output 7: float32 [2, 896, 4864], P(None, 'data')
- output 8: float32 [2, 4864, 896], P(None, 'data')
- output 9: float32 [], replicated
All inputs are finite; a program needn't handle non-finite values.
Results may differ from a plain program's by a relative error of at most 0.0109783.
Values are sent between devices in bfloat16 or wider.
A program may use at most 1 GiB of HBM per device.

v0:
```python
import jax
import jax.numpy as jnp
from jax import lax
from jax.sharding import PartitionSpec as P

BETA1 = 0.9
BETA2 = 0.95
ADAM_EPS = 1e-8
LEARN_RATE = 5e-3
NORM_EPS = 1e-6
STEP = 10
BIAS_ONE = 1.0 - BETA1 ** STEP
BIAS_TWO = 1.0 - BETA2 ** STEP


def gelu_value(pre_act):
    return pre_act * (0.5 + 0.5 * lax.erf(pre_act * 0.7071067811865476))


def gelu_slope(pre_act):
    return 0.5 + 0.5 * lax.erf(pre_act * 0.7071067811865476) + pre_act * jnp.exp(-0.5 * pre_act * pre_act) * 0.3989422804014327


def local_backward(inp_rows, out_grad, w_up, w_down):
    up_one = w_up[0]
    up_two = w_up[1]
    down_one = w_down[0]
    down_two = w_down[1]
    pre_one = jnp.dot(inp_rows, up_one, preferred_element_type=jnp.float32).astype(jnp.bfloat16)
    act_one = gelu_value(pre_one.astype(jnp.float32)).astype(jnp.bfloat16)
    mid_rows = jnp.dot(act_one, down_one, preferred_element_type=jnp.float32).astype(jnp.bfloat16)
    pre_two = jnp.dot(mid_rows, up_two, preferred_element_type=jnp.float32).astype(jnp.bfloat16)
    act_two = gelu_value(pre_two.astype(jnp.float32)).astype(jnp.bfloat16)
    grad_down2 = jnp.einsum('bf,bd->fd', act_two, out_grad, preferred_element_type=jnp.float32)
    dact_two = jnp.einsum('bd,fd->bf', out_grad, down_two, preferred_element_type=jnp.float32).astype(jnp.bfloat16)
    dpre_two = (dact_two.astype(jnp.float32) * gelu_slope(pre_two.astype(jnp.float32))).astype(jnp.bfloat16)
    grad_up2 = jnp.einsum('bd,bf->df', mid_rows, dpre_two, preferred_element_type=jnp.float32)
    dmid_rows = jnp.einsum('bf,df->bd', dpre_two, up_two, preferred_element_type=jnp.float32).astype(jnp.bfloat16)
    grad_down1 = jnp.einsum('bf,bd->fd', act_one, dmid_rows, preferred_element_type=jnp.float32)
    dact_one = jnp.einsum('bd,fd->bf', dmid_rows, down_one, preferred_element_type=jnp.float32).astype(jnp.bfloat16)
    dpre_one = (dact_one.astype(jnp.float32) * gelu_slope(pre_one.astype(jnp.float32))).astype(jnp.bfloat16)
    grad_up1 = jnp.einsum('bd,bf->df', inp_rows, dpre_one, preferred_element_type=jnp.float32)
    return grad_down2, grad_up2, grad_down1, grad_up1


def adam_update(grad_vals, master_vals, mom_vals, var_vals, clip_scale):
    new_mom = BETA1 * mom_vals + (1.0 - BETA1) * clip_scale * grad_vals
    new_var = BETA2 * var_vals + (1.0 - BETA2) * (clip_scale * clip_scale) * (grad_vals * grad_vals)
    new_master = master_vals - LEARN_RATE * (new_mom / BIAS_ONE) / (jnp.sqrt(new_var / BIAS_TWO) + ADAM_EPS)
    return new_master, new_mom, new_var


def solution(mesh):
    total_devices = mesh.shape['replica'] * mesh.shape['data']
    batch_spec = P(('replica', 'data'), None)
    whole_spec = P()
    shard_spec = P(None, 'data', None)

    def device_step(inp_rows, out_grad, w_up, w_down, master_up, master_down, mom_up, mom_down, var_up, var_down, clip_norm):
        grad_down2, grad_up2, grad_down1, grad_up1 = local_backward(inp_rows, out_grad, w_up, w_down)
        shard_down2 = lax.psum_scatter(grad_down2, 'data', scatter_dimension=0, tiled=True)
        shard_up2 = lax.psum_scatter(grad_up2, 'data', scatter_dimension=0, tiled=True)
        shard_down1 = lax.psum_scatter(grad_down1, 'data', scatter_dimension=0, tiled=True)
        shard_up1 = lax.psum_scatter(grad_up1, 'data', scatter_dimension=0, tiled=True)
        grad_up = lax.psum(jnp.stack([shard_up1, shard_up2]), 'replica') / total_devices
        grad_down = lax.psum(jnp.stack([shard_down1, shard_down2]), 'replica') / total_devices
        local_sq = jnp.sum(grad_up * grad_up) + jnp.sum(grad_down * grad_down)
        grad_norm = jnp.sqrt(lax.psum(local_sq, 'data'))
        clip_scale = jnp.minimum(1.0, clip_norm / (grad_norm + NORM_EPS))
        master_up_new, mom_up_new, var_up_new = adam_update(grad_up, master_up, mom_up, var_up, clip_scale)
        master_down_new, mom_down_new, var_down_new = adam_update(grad_down, master_down, mom_down, var_down, clip_scale)
        w_up_new = lax.all_gather(master_up_new.astype(jnp.bfloat16), 'data', axis=1, tiled=True)
        w_down_new = lax.all_gather(master_down_new.astype(jnp.bfloat16), 'data', axis=1, tiled=True)
        return (w_up_new, w_down_new, master_up_new, master_down_new, mom_up_new, mom_down_new, var_up_new, var_down_new, grad_norm)

    return jax.shard_map(device_step, mesh=mesh, in_specs=(batch_spec, batch_spec, whole_spec, whole_spec, shard_spec, shard_spec, shard_spec, shard_spec, shard_spec, shard_spec, whole_spec), out_specs=(whole_spec, whole_spec, shard_spec, shard_spec, shard_spec, shard_spec, shard_spec, shard_spec, whole_spec), check_vma=False)
```

profile of v0, /device:TPU:0, one launch (start us, length us, event | category | flops | bytes accessed | tf_op | source)
XLA Modules:
  0.0 1218.4 jit_solution(13378751237595873856)
XLA Ops:
  7.2 57.1 %fusion.2 = (f32[4096,4864]{1,0:T(8,128)}, bf16[4096,4864]{1,0:T(8,128)(2,1)}) fusion(bf16[4096,896]{1,0:T(8,128)(2,1)} %param.11, bf16[2,896,4864]{2,1,0:T(8,128)(2,1)} %param.13), kind=kOutput, calls=%fused_computation.12 | convolution fusion | flops 35801530368 | bytes 135593984 | tf_op jit(solution)/shard_map/dot_general | solution.py:29
  64.3 52.7 %fusion.40 = bf16[4096,896]{1,0:T(8,128)(2,1)} fusion(bf16[2,4864,896]{2,1,0:T(8,128)(2,1)} %param.14, f32[4096,4864]{1,0:T(8,128)} %get-tuple-element.37, bf16[4096,4864]{1,0:T(8,128)(2,1)} %get-tuple-element.38), kind=kOutput, calls=%fused_computation.48 | convolution fusion | flops 35765354496 | bytes 135593984 | tf_op jit(solution)/shard_map/dot_general | solution.py:31
  117.0 50.2 %convolution_convert_fusion = bf16[4096,4864]{1,0:T(8,128)(2,1)} fusion(bf16[4096,896]{1,0:T(8,128)(2,1)} %fusion.40, bf16[2,896,4864]{2,1,0:T(8,128)(2,1)} %param.13), kind=kOutput, calls=%fused_computation.30 | convolution fusion | flops 35721838592 | bytes 55902208 | tf_op jit(solution)/shard_map/dot_general | solution.py:32
  167.2 70.2 %fusion.16 = bf16[4096,4864]{1,0:T(8,128)(2,1)} fusion(bf16[4096,4864]{1,0:T(8,128)(2,1)} %convolution_convert_fusion, bf16[4096,896]{1,0:T(8,128)(2,1)} %param.12, bf16[2,4864,896]{2,1,0:T(8,128)(2,1)} %param.14), kind=kOutput, calls=%fused_computation.26 | convolution fusion | flops 35960913920 | bytes 95748096 | tf_op jit(solution)/shard_map/bd,fd->bf/dot_general | solution.py:35
  237.5 45.5 %fusion.56 = f32[896,4864]{1,0:T(8,128)} fusion(bf16[4096,896]{1,0:T(8,128)(2,1)S(1)} %copy-done, bf16[4096,4864]{1,0:T(8,128)(2,1)} %fusion.16), kind=kOutput, calls=%fused_computation.67 | convolution fusion | flops 35701915648 | bytes 64618496
  283.0 54.4 %fusion.18 = f32[4864,896]{1,0:T(8,128)} fusion(bf16[4096,896]{1,0:T(8,128)(2,1)} %param.12, bf16[4096,4864]{1,0:T(8,128)(2,1)} %convolution_convert_fusion), kind=kOutput, calls=%fused_computation.28 | convolution fusion | flops 35821453312 | bytes 64618496 | tf_op jit(solution)/shard_map/bf,bd->fd/dot_general | solution.py:34
  337.5 49.4 %fusion.43 = bf16[4096,896]{1,0:T(8,128)(2,1)} fusion(bf16[4096,4864]{1,0:T(8,128)(2,1)} %fusion.16, bf16[2,896,4864]{2,1,0:T(8,128)(2,1)} %param.13), kind=kOutput, calls=%fused_computation.49 | convolution fusion | flops 35705585664 | bytes 55902208 | tf_op jit(solution)/shard_map/bf,df->bd/dot_general | solution.py:38
  386.9 56.2 %fusion.50 = f32[4864,896]{1,0:T(8,128)} fusion(bf16[4096,896]{1,0:T(8,128)(2,1)} %fusion.43, f32[4096,4864]{1,0:T(8,128)} %get-tuple-element.37, bf16[4096,4864]{1,0:T(8,128)(2,1)} %get-tuple-element.38), kind=kOutput, calls=%fused_computation.64 | convolution fusion | flops 35761684480 | bytes 144310272 | tf_op jit(solution)/shard_map/bf,bd->fd/dot_general | solution.py:39
  443.2 49.9 %fusion.28 = bf16[4096,4864]{1,0:T(8,128)(2,1)} fusion(bf16[4096,896]{1,0:T(8,128)(2,1)} %fusion.43, bf16[2,4864,896]{2,1,0:T(8,128)(2,1)} %param.14), kind=kOutput, calls=%fused_computation.36 | convolution fusion | flops 35701915648 | bytes 55902208 | tf_op jit(solution)/shard_map/bd,fd->bf/dot_general | solution.py:40
  493.1 66.8 %fusion.22 = f32[896,4864]{0,1:T(8,128)} fusion(bf16[4096,896]{1,0:T(8,128)(2,1)} %param.11, f32[4096,4864]{1,0:T(8,128)} %get-tuple-element.37, bf16[4096,4864]{1,0:T(8,128)(2,1)} %get-tuple-element.38, bf16[4096,4864]{1,0:T(8,128)(2,1)} %fusion.28), kind=kOutput, calls=%fused_computation.32 | convolution fusion | flops 35881222144 | bytes 184156160 | tf_op jit(solution)/shard_map/bd,bf->df/dot_general | solution.py:42
  559.9 19.0 %copy.38 = f32[896,4864]{1,0:T(8,128)} copy(f32[896,4864]{0,1:T(8,128)} %fusion.22) | data formatting | bytes 34865152
  581.1 50.9 %reduce-scatter.9.cloned.1.call-done = f32[608,896]{1,0:T(8,128)} async-done(((f32[4864,896]{1,0:T(8,128)}), f32[608,896]{1,0:T(8,128)}) %reduce-scatter.9.cloned.1.call-update) | async-done | bytes 2179088 | tf_op jit(solution)/shard_map/reduce_scatter | solution.py:63
  632.0 4.6 pad_maximum_fusion.1
  636.6 111.8 %reduce-scatter.13.cloned.1.call-done = f32[112,4864]{1,0:T(8,128)} async-done(((f32[896,4864]{1,0:T(8,128)}), f32[112,4864]{1,0:T(8,128)}) %reduce-scatter.13.cloned.1.call-update) | async-done | bytes 2179088
  751.5 4.3 pad_maximum_fusion
  756.5 5.8 copy.31
  762.3 5.6 copy.28
  767.9 202.6 %all-reduce.3.cloned.1.call-done = (f32[2,112,4864]{1,2,0:T(8,128)}, f32[2,608,896]{2,1,0:T(8,128)}) async-done(((f32[2,112,4864]{1,2,0:T(8,128)}, f32[2,608,896]{2,1,0:T(8,128)}), (f32[2,112,4864]{1,2,0:T(8,128)}, f32[2,608,896]{2,1,0:T(8,128)})) %all-reduce.3.cloned.1.call-update) | async-done | bytes 8716304 | tf_op jit(solution)/shard_map/psum | solution.py:65
  970.5 4.0 fusion.47
  974.4 4.3 fusion.46
  980.0 5.6 copy.30
  985.6 13.8 %psum.23 = f32[]{:T(128)} all-reduce(f32[]{:T(128)S(6)} %add.62), channel_id=1, replica_groups=mesh['replica'=2,'data'=8] {'data'}, use_global_device_ids=true, to_apply=%region_8.0 | all-reduce | flops 1 | bytes 8 | tf_op jit(solution)/shard_map/psum | solution.py:68
  1000.2 13.5 %fusion.55 = (bf16[2,112,4864]{1,2,0:T(8,128)(2,1)S(1)}, f32[2,112,4864]{1,2,0:T(8,128)}, f32[2,112,4864]{1,2,0:T(8,128)}, f32[2,112,4864]{1,2,0:T(8,128)}) fusion(f32[2,112,4864]{1,2,0:T(8,128)} %copy.31, f32[2,112,4864]{1,2,0:T(8,128)} %get-tuple-element.27, f32[]{:T(128)S(6)} %mul.152, f32[2,112,4864]{1,2,0:T(8,128)} %copy.28, f32[]{:T(128)S(6)} %mul.160, ...), kind=kLoop, calls=%fused_computation.66 | loop fusion | flops 15253504 | bytes 32686088 | tf_op jit(solution)/shard_map/convert_element_type | solution.py:72
  1013.7 4.7 copy.32
  1018.4 12.5 %fusion.54 = (bf16[2,608,896]{2,1,0:T(8,128)(2,1)}, f32[2,608,896]{2,1,0:T(8,128)}, f32[2,608,896]{2,1,0:T(8,128)}, f32[2,608,896]{2,1,0:T(8,128)}) fusion(f32[2,608,896]{2,1,0:T(8,128)} %param.16, f32[2,608,896]{2,1,0:T(8,128)} %get-tuple-element.28, f32[]{:T(128)S(6)} %mul.152, f32[2,608,896]{2,1,0:T(8,128)} %param.18, f32[]{:T(128)S(6)} %mul.160, ...), kind=kLoop, calls=%fused_computation.65 | loop fusion | flops 15253504 | bytes 32686088 | tf_op jit(solution)/shard_map/convert_element_type | solution.py:73
  1031.0 5.6 copy.34
  1036.6 5.6 copy.35
  1042.2 5.6 copy.36
  1047.7 57.7 %all-gather.3.cloned.1.call-done = bf16[2,896,4864]{2,0,1:T(2,128)(2,1)} async-done(((bf16[2,112,4864]{2,0,1:T(2,128)(2,1)}), bf16[2,896,4864]{2,0,1:T(2,128)(2,1)}) %all-gather.3.cloned.1.call-update) | async-done | bytes 17432592 | tf_op jit(solution)/shard_map/all_gather | solution.py:72
  1105.4 15.6 %copy.33 = bf16[2,896,4864]{2,1,0:T(8,128)(2,1)} copy(bf16[2,896,4864]{2,0,1:T(2,128)(2,1)} %all-gather.3.cloned.1.call-done) | data formatting | bytes 34865152
  1121.0 75.0 %all-gather.5.cloned.1.call-done = bf16[2,4864,896]{2,1,0:T(8,128)(2,1)} async-done(((bf16[2,608,896]{2,1,0:T(8,128)(2,1)}), bf16[2,4864,896]{2,1,0:T(8,128)(2,1)}) %all-gather.5.cloned.1.call-update) | async-done | bytes 17432592 | tf_op jit(solution)/shard_map/all_gather | solution.py:73
  1195.9 14.3 %copy.46 = bf16[2,4864,896]{2,1,0:T(8,128)(2,1)} copy(bf16[2,4864,896]{2,1,0:T(8,128)(2,1)} %all-gather.5.cloned.1.call-done) | data formatting | bytes 34865152
  (20 shorter events, 5.6 us)
Async XLA Ops:
  7.2 571.8 %reduce-scatter.15.cloned.1.call-start = ((), (), s32[]{:S(2)}) async-start(), calls=%async_computation.9 | async-start | bytes 19611648
  167.2 70.3 %copy-start = (bf16[4096,896]{1,0:T(8,128)(2,1)S(1)}, bf16[4096,896]{1,0:T(8,128)(2,1)}, u32[]{:S(2)}) copy-start(bf16[4096,896]{1,0:T(8,128)(2,1)} %fusion.40) | copy-start | bytes 22020100
  283.0 298.1 %reduce-scatter.11.cloned.1.call-start = ((), (), s32[]{:S(2)}) async-start(), calls=%async_computation.5 | async-start | bytes 19611648 | tf_op jit(solution)/shard_map/reduce_scatter | solution.py:61
  337.5 294.5 %reduce-scatter.9.cloned.1.call-start = ((), (), s32[]{:S(2)}) async-start(), calls=%async_computation.4 | async-start | bytes 19611648 | tf_op jit(solution)/shard_map/reduce_scatter | solution.py:63
  443.2 305.2 %reduce-scatter.13.cloned.1.call-start = ((), (), s32[]{:S(2)}) async-start(), calls=%async_computation.8 | async-start | bytes 19611648
  578.9 391.5 %all-reduce.3.cloned.1.call-start = ((), (), s32[]{:S(2)}) async-start(), calls=%async_computation.10 | async-start | bytes 18677760 | tf_op jit(solution)/shard_map/psum | solution.py:65
  755.8 349.6 %all-gather.3.cloned.1.call-start = ((), (), s32[]{:S(2)}) async-start(), calls=%async_computation.6 | async-start | bytes 19611648 | tf_op jit(solution)/shard_map/all_gather | solution.py:72
  1018.4 177.6 %all-gather.5.cloned.1.call-start = ((), (), s32[]{:S(2)}) async-start(), calls=%async_computation.7 | async-start | bytes 19611648 | tf_op jit(solution)/shard_map/all_gather | solution.py:73
Sparse Core Ops, SparseCore 0:
  283.1 115.7 reduce-scatter.14
  402.5 112.8 reduce-scatter.10
  519.0 112.8 reduce-scatter.8
  635.5 112.8 reduce-scatter.12
  755.9 214.4 all-reduce.2
  1018.5 86.8 all-gather.2
  1107.2 88.6 all-gather.4
where the time goes:
time: 1230 us; the launch traced here: 1220 us
  matrix products  552 us (45%)
  waiting for transfers between devices  498 us (40%)
  local copies, waits for them, and re-layouts  92.4 us (8%)
  other arithmetic  43.2 us (4%)
  between operations  18.2 us (1%)
  blocking collectives  13.8 us (1%)
    psum x1, waiting for transfers between devices, device_step(): lax.psum(jnp.stack([shard_up1, shard_up2]), 'replica') / total_devices  203 us
    unnamed x9, waiting for transfers between devices  112 us
    unnamed x13, local copies, waits for them, and re-layouts  87.7 us
    all_gather x1, waiting for transfers between devices, device_step(): lax.all_gather(master_down_new.astype(jnp.bfloat16), 'data', axis=1, tile...  75 us
    dot_general x1, matrix products, local_backward(): jnp.einsum('bd,fd->bf', out_grad, down_two, preferred_element_type=jnp.fl...  70.2 us
    dot_general x1, matrix products, local_backward(): jnp.einsum('bd,bf->df', inp_rows, dpre_one, preferred_element_type=jnp.fl...  66.8 us
    all_gather x1, waiting for transfers between devices, device_step(): lax.all_gather(master_up_new.astype(jnp.bfloat16), 'data', axis=1, tiled=...  57.7 us
    dot_general x1, matrix products, local_backward(): jnp.dot(inp_rows, up_one, preferred_element_type=jnp.float32)  57.1 us
  transfers between devices with their start and end apart: 7, of which 5 were waited for; matrix products, arithmetic and copies ran while one was open for 29% of the time, Pallas kernels for 0%

commit v1 on v0

v1 whole, which is shorter than its diff:
```python
import functools

import jax
import jax.numpy as jnp
from jax import lax
from jax.experimental import pallas as pl
from jax.experimental.pallas import tpu as pltpu
from jax.sharding import PartitionSpec as P

BETA1 = 0.9
BETA2 = 0.95
ADAM_EPS = 1e-8
LEARN_RATE = 5e-3
NORM_EPS = 1e-6
STEP = 10
BIAS_ONE = 1.0 - BETA1 ** STEP
BIAS_TWO = 1.0 - BETA2 ** STEP

F32 = jnp.float32
BF16 = jnp.bfloat16
ROWS = 4096
D = 896
FF = 4864
TILE = 256
NT = FF // TILE
OWN = 8
PIECE = TILE // OWN
RM = 1024
VMEM_LIMIT = 67_043_328


def gelu_value(pre_act):
    return pre_act * (0.5 + 0.5 * lax.erf(pre_act * 0.7071067811865476))


def gelu_both(pre_act):
    cdf = 0.5 + 0.5 * lax.erf(pre_act * 0.7071067811865476)
    return pre_act * cdf, cdf + pre_act * jnp.exp(-0.5 * pre_act * pre_act) * 0.3989422804014327


def mm(left, right):
    return jnp.dot(left, right, preferred_element_type=F32)


def mm_nt(left, right):
    return lax.dot_general(left, right, (((1,), (1,)), ((), ())), preferred_element_type=F32)


def permute_kernel(w_ref, out_ref):
    for t in range(NT):
        out_ref[:, t * TILE:(t + 1) * TILE] = jnp.concatenate(
            [w_ref[:, d * (FF // OWN) + t * PIECE:d * (FF // OWN) + (t + 1) * PIECE] for d in range(OWN)], axis=1)


def permute_columns(w_up):
    rows = 128
    flat = w_up.reshape(2 * D, FF)
    out = pl.pallas_call(
        permute_kernel,
        grid=(2 * D // rows,),
        in_specs=[pl.BlockSpec((rows, FF), lambda i: (i, 0))],
        out_specs=pl.BlockSpec((rows, FF), lambda i: (i, 0)),
        out_shape=jax.ShapeDtypeStruct((2 * D, FF), w_up.dtype),
        name="permute_columns",
    )(flat)
    return out.reshape(2, D, FF)


def forward_kernel(x_ref, wu_ref, wd_ref, z_ref, h_ref, acc):
    t = pl.program_id(0)

    @pl.when(t == 0)
    def _():
        acc[...] = jnp.zeros_like(acc)

    wd = wd_ref[0, :, 0].reshape(TILE, D)

    def body(r, carry):
        rows = pl.ds(pl.multiple_of(r * RM, RM), RM)
        z = mm(x_ref[rows, :], wu_ref[0]).astype(BF16)
        z_ref[0, rows, :] = z
        u = gelu_value(z.astype(F32)).astype(BF16)
        acc[rows, :] += mm(u, wd)
        return carry

    lax.fori_loop(0, ROWS // RM, body, 0)

    @pl.when(t == NT - 1)
    def _():
        h_ref[...] = acc[...].astype(BF16)


def forward(x, w_upp, w_down5):
    return pl.pallas_call(
        forward_kernel,
        grid=(NT,),
        in_specs=[
            pl.BlockSpec((ROWS, D), lambda t: (0, 0), pipeline_mode=pl.Buffered(1)),
            pl.BlockSpec((1, D, TILE), lambda t: (0, 0, t)),
            pl.BlockSpec((1, OWN, 1, PIECE, D), lambda t: (0, 0, t, 0, 0)),
        ],
        out_specs=[
            pl.BlockSpec((1, ROWS, TILE), lambda t: (t, 0, 0)),
            pl.BlockSpec((ROWS, D), lambda t: (0, 0), pipeline_mode=pl.Buffered(1)),
        ],
        out_shape=[jax.ShapeDtypeStruct((NT, ROWS, TILE), BF16), jax.ShapeDtypeStruct((ROWS, D), BF16)],
        scratch_shapes=[pltpu.VMEM((ROWS, D), F32)],
        compiler_params=pltpu.CompilerParams(vmem_limit_bytes=VMEM_LIMIT),
        name="forward",
    )(x, w_upp, w_down5)


def upper_kernel(h_hbm, ht_hbm, dy_hbm, dyt_hbm, wu_ref, wd_ref, gd_ref, gu_ref, dh_hbm,
                 h, ht, dy, dyt, acc, u_s, d_s, sems):
    t = pl.program_id(0)
    loads = [pltpu.make_async_copy(s, v, sems.at[i]) for i, (s, v) in
             enumerate([(h_hbm, h), (dy_hbm, dy), (dyt_hbm, dyt), (ht_hbm, ht)])]

    @pl.when(t == 0)
    def _():
        for copy in loads:
            copy.start()
        acc[...] = jnp.zeros_like(acc)
        loads[0].wait()
        loads[1].wait()

    wu = wu_ref[0]
    wd = wd_ref[0, :, 0].reshape(TILE, D)

    def body(r, carry):
        rows = pl.ds(pl.multiple_of(r * RM, RM), RM)
        z = mm(h[rows, :], wu).astype(BF16).astype(F32)
        e = mm_nt(dy[rows, :], wd).astype(BF16).astype(F32)
        u, slope = gelu_both(z)
        u_s[rows, :] = u.astype(BF16)
        dz = (e * slope).astype(BF16)
        d_s[rows, :] = dz
        acc[rows, :] += mm_nt(dz, wu)
        return carry

    lax.fori_loop(0, ROWS // RM, body, 0)

    @pl.when(t == 0)
    def _():
        loads[2].wait()
        loads[3].wait()

    gd_ref[:, 0] = mm(dyt[...], u_s[...]).T.reshape(OWN, PIECE, D)
    gu_ref[...] = mm(ht[...], d_s[...])

    @pl.when(t == NT - 1)
    def _():
        h[...] = acc[...].astype(BF16)
        out = pltpu.make_async_copy(h, dh_hbm, sems.at[0])
        out.start()
        out.wait()


def upper(h, ht, dy, dyt, w_upp, w_down5):
    anyspec = pl.BlockSpec(memory_space=pl.ANY)
    return pl.pallas_call(
        upper_kernel,
        grid=(NT,),
        in_specs=[anyspec] * 4 + [
            pl.BlockSpec((1, D, TILE), lambda t: (1, 0, t)),
            pl.BlockSpec((1, OWN, 1, PIECE, D), lambda t: (1, 0, t, 0, 0)),
        ],
        out_specs=[
            pl.BlockSpec((OWN, 1, PIECE, D), lambda t: (0, t, 0, 0)),
            pl.BlockSpec((D, TILE), lambda t: (0, t)),
            anyspec,
        ],
        out_shape=[jax.ShapeDtypeStruct((OWN, NT, PIECE, D), F32), jax.ShapeDtypeStruct((D, FF), F32),
                   jax.ShapeDtypeStruct((ROWS, D), BF16)],
        scratch_shapes=[pltpu.VMEM((ROWS, D), BF16), pltpu.VMEM((D, ROWS), BF16),
                        pltpu.VMEM((ROWS, D), BF16), pltpu.VMEM((D, ROWS), BF16),
                        pltpu.VMEM((ROWS, D), F32), pltpu.VMEM((ROWS, TILE), BF16), pltpu.VMEM((ROWS, TILE), BF16),
                        pltpu.SemaphoreType.DMA((4,))],
        compiler_params=pltpu.CompilerParams(vmem_limit_bytes=VMEM_LIMIT),
        name="upper",
    )(h, ht, dy, dyt, w_upp, w_down5)


def lower_kernel(dh_hbm, dht_hbm, xt_hbm, z_ref, wd_ref, gd_ref, gu_ref,
                 dh, dht, xt, u_s, d_s, sems):
    t = pl.program_id(0)
    loads = [pltpu.make_async_copy(s, v, sems.at[i]) for i, (s, v) in
             enumerate([(dh_hbm, dh), (dht_hbm, dht), (xt_hbm, xt)])]

    @pl.when(t == 0)
    def _():
        for copy in loads:
            copy.start()
        loads[0].wait()

    wd = wd_ref[0, :, 0].reshape(TILE, D)

    def body(r, carry):
        rows = pl.ds(pl.multiple_of(r * RM, RM), RM)
        z = z_ref[0, rows, :].astype(F32)
        e = mm_nt(dh[rows, :], wd).astype(BF16).astype(F32)
        u, slope = gelu_both(z)
        u_s[rows, :] = u.astype(BF16)
        d_s[rows, :] = (e * slope).astype(BF16)
        return carry

    lax.fori_loop(0, ROWS // RM, body, 0)

    @pl.when(t == 0)
    def _():
        loads[1].wait()
        loads[2].wait()

    gd_ref[:, 0] = mm(dht[...], u_s[...]).T.reshape(OWN, PIECE, D)
    gu_ref[...] = mm(xt[...], d_s[...])


def lower(dh, dht, xt, z, w_down5):
    anyspec = pl.BlockSpec(memory_space=pl.ANY)
    return pl.pallas_call(
        lower_kernel,
        grid=(NT,),
        in_specs=[anyspec] * 3 + [
            pl.BlockSpec((1, ROWS, TILE), lambda t: (t, 0, 0)),
            pl.BlockSpec((1, OWN, 1, PIECE, D), lambda t: (0, 0, t, 0, 0)),
        ],
        out_specs=[
            pl.BlockSpec((OWN, 1, PIECE, D), lambda t: (0, t, 0, 0)),
            pl.BlockSpec((D, TILE), lambda t: (0, t)),
        ],
        out_shape=[jax.ShapeDtypeStruct((OWN, NT, PIECE, D), F32), jax.ShapeDtypeStruct((D, FF), F32)],
        scratch_shapes=[pltpu.VMEM((ROWS, D), BF16), pltpu.VMEM((D, ROWS), BF16), pltpu.VMEM((D, ROWS), BF16),
                        pltpu.VMEM((ROWS, TILE), BF16), pltpu.VMEM((ROWS, TILE), BF16),
                        pltpu.SemaphoreType.DMA((3,))],
        compiler_params=pltpu.CompilerParams(vmem_limit_bytes=VMEM_LIMIT),
        name="lower",
    )(dh, dht, xt, z, w_down5)


def adam_update(grad_vals, master_vals, mom_vals, var_vals, clip_scale):
    new_mom = BETA1 * mom_vals + (1.0 - BETA1) * clip_scale * grad_vals
    new_var = BETA2 * var_vals + (1.0 - BETA2) * (clip_scale * clip_scale) * (grad_vals * grad_vals)
    new_master = master_vals - LEARN_RATE * (new_mom / BIAS_ONE) / (jnp.sqrt(new_var / BIAS_TWO) + ADAM_EPS)
    return new_master, new_mom, new_var


def unpermute(shard):
    rows = shard.shape[0]
    return shard.reshape(rows, NT, OWN, PIECE).transpose(0, 2, 1, 3).reshape(rows, FF)


def solution(mesh):
    total_devices = mesh.shape['replica'] * mesh.shape['data']
    batch_spec = P(('replica', 'data'), None)
    whole_spec = P()
    shard_spec = P(None, 'data', None)

    def device_step(inp_rows, out_grad, w_up, w_down, master_up, master_down, mom_up, mom_down, var_up, var_down, clip_norm):
        w_upp = permute_columns(w_up)
        w_down5 = w_down.reshape(2, OWN, NT, PIECE, D)
        pre_one, mid_rows = forward(inp_rows, w_upp, w_down5)
        grad_down2, grad_up2, dmid_rows = upper(mid_rows, mid_rows.T, out_grad, out_grad.T, w_upp, w_down5)
        grad_down1, grad_up1 = lower(dmid_rows, dmid_rows.T, inp_rows.T, pre_one, w_down5)
        grad_down2 = grad_down2.reshape(FF, D)
        grad_down1 = grad_down1.reshape(FF, D)
        shard_down2 = lax.psum_scatter(grad_down2, 'data', scatter_dimension=0, tiled=True)
        shard_up2 = lax.psum_scatter(grad_up2, 'data', scatter_dimension=0, tiled=True)
        shard_down1 = lax.psum_scatter(grad_down1, 'data', scatter_dimension=0, tiled=True)
        shard_up1 = lax.psum_scatter(grad_up1, 'data', scatter_dimension=0, tiled=True)
        shard_up1 = unpermute(shard_up1)
        shard_up2 = unpermute(shard_up2)
        grad_up = lax.psum(jnp.stack([shard_up1, shard_up2]), 'replica') / total_devices
        grad_down = lax.psum(jnp.stack([shard_down1, shard_down2]), 'replica') / total_devices
        local_sq = jnp.sum(grad_up * grad_up) + jnp.sum(grad_down * grad_down)
        grad_norm = jnp.sqrt(lax.psum(local_sq, 'data'))
        clip_scale = jnp.minimum(1.0, clip_norm / (grad_norm + NORM_EPS))
        master_up_new, mom_up_new, var_up_new = adam_update(grad_up, master_up, mom_up, var_up, clip_scale)
        master_down_new, mom_down_new, var_down_new = adam_update(grad_down, master_down, mom_down, var_down, clip_scale)
        w_up_new = lax.all_gather(master_up_new.astype(jnp.bfloat16), 'data', axis=1, tiled=True)
        w_down_new = lax.all_gather(master_down_new.astype(jnp.bfloat16), 'data', axis=1, tiled=True)
        return (w_up_new, w_down_new, master_up_new, master_down_new, mom_up_new, mom_down_new, var_up_new, var_down_new, grad_norm)

    return jax.shard_map(device_step, mesh=mesh, in_specs=(batch_spec, batch_spec, whole_spec, whole_spec, shard_spec, shard_spec, shard_spec, shard_spec, shard_spec, shard_spec, whole_spec), out_specs=(whole_spec, whole_spec, shard_spec, shard_spec, shard_spec, shard_spec, shard_spec, shard_spec, whole_spec), check_vma=False)
```

time: 1230 us -> 1480 us (1.20)
  Pallas kernels: 0 us -> 617 us
  matrix products: 552 us -> 0 us
  waiting for transfers between devices: 498 us -> 672 us
  local copies, waits for them, and re-layouts: 92.4 us -> 121 us
    pallas_call x0 -> x4, Pallas kernels: none -> 617 us  [the longest x1 255 us: upper(): pl.pallas_call(upper_kernel, grid=(NT,), in_specs=[anyspec] * 4 + [pl.Blo...]
    dot_general x9 -> x0, matrix products: 507 us -> none  [the longest x1 70.2 us: local_backward(): jnp.einsum('bd,fd->bf', out_grad, down_two, preferred_element_type=jnp.fl...]
    unnamed x9 -> x7, waiting for transfers between devices: 112 us -> 1.29 us
    reduce_scatter x1, waiting for transfers between devices: 0.02 us -> 110 us  [device_step(): lax.psum_scatter(grad_down2, 'data', scatter_dimension=0, tiled=True)]
    reduce_scatter x0 -> x2, waiting for transfers between devices: none -> 109 us  [the longest x1 109 us: device_step(): lax.psum_scatter(grad_up1, 'data', scatter_dimension=0, tiled=True)]
    reduce_scatter x1, waiting for transfers between devices: 50.9 us -> 117 us  [device_step(): lax.psum_scatter(grad_down1, 'data', scatter_dimension=0, tiled=True)]
    unnamed x1 -> x0, matrix products: 45.5 us -> none
    pallas_call x0 -> x2, local copies, waits for them, and re-layouts: none -> 21.4 us  [the longest x1 10.7 us: forward(): pl.pallas_call(forward_kernel, grid=(NT,), in_specs=[pl.BlockSpec((ROWS,...]
  transfers between devices with their start and end apart: 7 -> 7, of which waited for: 5 -> 6; matrix products, arithmetic and copies ran while one was open for 29% -> 6% of each run, Pallas kernels for 0% -> 11%
where the time goes in v1:
time: 1480 us
  waiting for transfers between devices  672 us (45%)
  Pallas kernels  617 us (42%)
  local copies, waits for them, and re-layouts  121 us (8%)
  other arithmetic  39.4 us (3%)
  between operations  18 us (1%)
    pallas_call x1, Pallas kernels, upper(): pl.pallas_call(upper_kernel, grid=(NT,), in_specs=[anyspec] * 4 + [pl.Blo...  255 us
    psum x1, waiting for transfers between devices, device_step(): lax.psum(jnp.stack([shard_up1, shard_up2]), 'replica') / total_devices  203 us
    pallas_call x1, Pallas kernels, forward(): pl.pallas_call(forward_kernel, grid=(NT,), in_specs=[pl.BlockSpec((ROWS,...  180 us
    pallas_call x1, Pallas kernels, lower(): pl.pallas_call(lower_kernel, grid=(NT,), in_specs=[anyspec] * 3 + [pl.Blo...  160 us
    reduce_scatter x1, waiting for transfers between devices, device_step(): lax.psum_scatter(grad_down1, 'data', scatter_dimension=0, tiled=True)  117 us
    reduce_scatter x1, waiting for transfers between devices, device_step(): lax.psum_scatter(grad_down2, 'data', scatter_dimension=0, tiled=True)  110 us
    reduce_scatter x1, waiting for transfers between devices, device_step(): lax.psum_scatter(grad_up1, 'data', scatter_dimension=0, tiled=True)  109 us
    unnamed x12, local copies, waits for them, and re-layouts  84.9 us
  transfers between devices with their start and end apart: 7, of which 6 were waited for; matrix products, arithmetic and copies ran while one was open for 6% of the time, Pallas kernels for 11%

profile of v1, /device:TPU:0, one launch (start us, length us, event | category | flops | bytes accessed | tf_op | source)
XLA Modules:
  0.0 1482.2 jit_solution(46924893667169378)
XLA Ops:
  7.2 21.5 %permute_columns.1 = bf16[1792,4864]{1,0:T(8,128)(2,1)} custom-call(bf16[1792,4864]{1,0:T(8,128)(2,1)} %bitcast.28), custom_call_target="tpu_custom_call" | custom-call | tf_op jit(solution)/shard_map/permute_columns/pallas_call | solution.py:58
  28.7 180.0 %forward.1 = (bf16[19,4096,256]{2,1,0:T(8,128)(2,1)}, bf16[4096,896]{1,0:T(8,128)(2,1)}) custom-call(bf16[4096,896]{1,0:T(8,128)(2,1)} %x_ref.1, bf16[2,896,4864]{2,1,0:T(8,128)(2,1)} %bitcast.22, bf16[2,8,19,32,896]{4,3,2,1,0:T(8,128)(2,1)} %bitcast.19), custom_call_target="tpu_custom_call" | custom-call | tf_op jit(solution)/shard_map/forward/pallas_call | solution.py:94
  208.7 10.7 copy.42
  219.4 10.7 copy.43
  230.1 255.0 %upper.1 = (f32[8,19,32,896]{3,2,1,0:T(8,128)}, f32[896,4864]{1,0:T(8,128)}, bf16[4096,896]{1,0:T(8,128)(2,1)}) custom-call(bf16[4096,896]{1,0:T(8,128)(2,1)} %get-tuple-element.16.h_hbm, bf16[896,4096]{1,0:T(8,128)(2,1)} %bitcast.26, bf16[4096,896]{1,0:T(8,128)(2,1)} %dy_hbm.1, bf16[896,4096]{1,0:T(8,128)(2,1)} %bitcast.27, bf16[2,896,4864]{2,1,0:T(8,128)(2,1)} %bitcast.23, ...), custom_call_target="tpu_custom_call" | custom-call | tf_op jit(solution)/shard_map/upper/pallas_call | solution.py:161
  485.4 10.7 copy.45
  496.1 10.7 copy.44
  506.8 160.4 %lower.1 = (f32[8,19,32,896]{3,2,1,0:T(8,128)}, f32[896,4864]{1,0:T(8,128)}) custom-call(bf16[4096,896]{1,0:T(8,128)(2,1)} %get-tuple-element.17.dh_hbm, bf16[896,4096]{1,0:T(8,128)(2,1)} %bitcast.25, bf16[896,4096]{1,0:T(8,128)(2,1)} %bitcast.24, bf16[19,4096,256]{2,1,0:T(8,128)(2,1)} %get-tuple-element.18.z_ref, bf16[2,8,19,32,896]{4,3,2,1,0:T(8,128)(2,1)} %bitcast.21), custom_call_target="tpu_custom_call" | custom-call | tf_op jit(solution)/shard_map/lower/pallas_call | solution.py:220
  668.7 3.1 copy.48
  671.8 1.9 copy.49
  673.7 109.4 %reduce-scatter.5.cloned.1.call-done = f32[112,4864]{1,0:T(8,128)} async-done(((f32[896,4864]{1,0:T(8,128)}), f32[112,4864]{1,0:T(8,128)}) %reduce-scatter.5.cloned.1.call-update) | async-done | bytes 2179088 | tf_op jit(solution)/shard_map/reduce_scatter | solution.py:269
  783.2 3.1 copy.46
  788.2 2.6 pad_maximum_fusion
  790.8 109.5 %reduce-scatter.11.cloned.1.call-done = f32[608,896]{1,0:T(8,128)} async-done(((f32[4864,896]{1,0:T(8,128)}), f32[608,896]{1,0:T(8,128)}) %reduce-scatter.11.cloned.1.call-update) | async-done | bytes 2179088 | tf_op jit(solution)/shard_map/reduce_scatter | solution.py:266
  900.3 117.0 %reduce-scatter.9.cloned.1.call-done = f32[608,896]{1,0:T(8,128)} async-done(((f32[4864,896]{1,0:T(8,128)}), f32[608,896]{1,0:T(8,128)}) %reduce-scatter.9.cloned.1.call-update) | async-done | bytes 2179088 | tf_op jit(solution)/shard_map/reduce_scatter | solution.py:268
  1017.3 4.6 pad_maximum_fusion.1
  1022.0 5.6 copy.51
  1028.2 5.6 copy.41
  1033.9 202.7 %all-reduce.3.cloned.1.call-done = (f32[2,112,4864]{1,2,0:T(8,128)}, f32[2,608,896]{2,1,0:T(8,128)}) async-done(((f32[2,112,4864]{1,2,0:T(8,128)}, f32[2,608,896]{2,1,0:T(8,128)}), (f32[2,112,4864]{1,2,0:T(8,128)}, f32[2,608,896]{2,1,0:T(8,128)})) %all-reduce.3.cloned.1.call-update) | async-done | bytes 8716304 | tf_op jit(solution)/shard_map/psum | solution.py:272
  1236.5 4.4 fusion
  1244.0 5.6 copy.50
  1249.6 13.8 psum.23
  1264.2 13.5 fusion.3
  1277.6 4.8 copy.52
  1282.7 12.5 fusion.2
  1295.3 5.6 copy.54
  1300.9 5.6 copy.55
  1306.4 5.6 copy.56
  1312.0 57.4 %all-gather.3.cloned.1.call-done = bf16[2,896,4864]{2,0,1:T(2,128)(2,1)} async-done(((bf16[2,112,4864]{2,0,1:T(2,128)(2,1)}), bf16[2,896,4864]{2,0,1:T(2,128)(2,1)}) %all-gather.3.cloned.1.call-update) | async-done | bytes 17432592 | tf_op jit(solution)/shard_map/all_gather | solution.py:279
  1369.4 15.6 %copy.53 = bf16[2,896,4864]{2,1,0:T(8,128)(2,1)} copy(bf16[2,896,4864]{2,0,1:T(2,128)(2,1)} %all-gather.3.cloned.1.call-done) | data formatting | bytes 34865152
  1385.0 75.0 %all-gather.5.cloned.1.call-done = bf16[2,4864,896]{2,1,0:T(8,128)(2,1)} async-done(((bf16[2,608,896]{2,1,0:T(8,128)(2,1)}), bf16[2,4864,896]{2,1,0:T(8,128)(2,1)}) %all-gather.5.cloned.1.call-update) | async-done | bytes 17432592 | tf_op jit(solution)/shard_map/all_gather | solution.py:280
  1460.0 14.3 copy.61
  (19 shorter events, 5.6 us)
Async XLA Ops:
  7.2 661.5 %reduce-scatter.7.cloned.1.call-start = ((), (), s32[]{:S(2)}) async-start(), calls=%async_computation.5 | async-start | bytes 19611648 | tf_op jit(solution)/shard_map/reduce_scatter | solution.py:267
  485.2 298.0 %reduce-scatter.5.cloned.1.call-start = ((), (), s32[]{:S(2)}) async-start(), calls=%async_computation.4 | async-start | bytes 19611648 | tf_op jit(solution)/shard_map/reduce_scatter | solution.py:269
  667.3 233.0 %reduce-scatter.11.cloned.1.call-start = ((), (), s32[]{:S(2)}) async-start(), calls=%async_computation.7 | async-start | bytes 19611648 | tf_op jit(solution)/shard_map/reduce_scatter | solution.py:266
  668.0 349.3 %reduce-scatter.9.cloned.1.call-start = ((), (), s32[]{:S(2)}) async-start(), calls=%async_computation.6 | async-start | bytes 19611648 | tf_op jit(solution)/shard_map/reduce_scatter | solution.py:268
  668.6 568.0 %all-reduce.3.cloned.1.call-start = ((), (), s32[]{:S(2)}) async-start(), calls=%async_computation.10 | async-start | bytes 18677760 | tf_op jit(solution)/shard_map/psum | solution.py:272
  1021.9 347.5 %all-gather.3.cloned.1.call-start = ((), (), s32[]{:S(2)}) async-start(), calls=%async_computation.8 | async-start | bytes 19611648 | tf_op jit(solution)/shard_map/all_gather | solution.py:279
  1236.5 4.5 copy-start
  1282.4 177.6 %all-gather.5.cloned.1.call-start = ((), (), s32[]{:S(2)}) async-start(), calls=%async_computation.9 | async-start | bytes 19611648 | tf_op jit(solution)/shard_map/all_gather | solution.py:280
Sparse Core Ops, SparseCore 0:
  485.3 115.7 reduce-scatter.6
  667.4 115.7 reduce-scatter.4
  787.4 112.8 reduce-scatter.10
  904.3 112.8 reduce-scatter.8
  1022.0 214.4 all-reduce.2
  1282.5 86.8 all-gather.2
  1371.3 88.6 all-gather.4

commit v2 on v1

v2 whole, which is shorter than its diff:
```python
import functools

import jax
import jax.numpy as jnp
from jax import lax
from jax.experimental import pallas as pl
from jax.experimental.pallas import tpu as pltpu
from jax.sharding import PartitionSpec as P

BETA1 = 0.9
BETA2 = 0.95
ADAM_EPS = 1e-8
LEARN_RATE = 5e-3
NORM_EPS = 1e-6
STEP = 10
BIAS_ONE = 1.0 - BETA1 ** STEP
BIAS_TWO = 1.0 - BETA2 ** STEP

F32 = jnp.float32
BF16 = jnp.bfloat16
ROWS = 4096
D = 896
FF = 4864
TILE = 256
NT = FF // TILE
OWN = 8
PIECE = TILE // OWN
RM = 512
NB = ROWS // RM
VMEM_LIMIT = 67_043_328


def gelu_value(pre_act):
    return pre_act * (0.5 + 0.5 * lax.erf(pre_act * 0.7071067811865476))


def gelu_both(pre_act):
    cdf = 0.5 + 0.5 * lax.erf(pre_act * 0.7071067811865476)
    return pre_act * cdf, cdf + pre_act * jnp.exp(-0.5 * pre_act * pre_act) * 0.3989422804014327


def mm(left, right):
    return jnp.dot(left, right, preferred_element_type=F32)


def mm_nt(left, right):
    return lax.dot_general(left, right, (((1,), (1,)), ((), ())), preferred_element_type=F32)


MESH = pl.DeviceIdType.MESH
LAG = 4
GRID = NT + LAG


def coordinates():
    d = lax.axis_index('data')
    z = lax.axis_index('replica')
    c = lax.rem(d, 2)
    x = lax.rem(lax.div(d, 2), 2)
    y = lax.div(d, 4)
    peers = {
        'c': {'data': d + 1 - 2 * c},
        'x': {'data': d + 2 - 4 * x},
        'y': {'data': d + 4 - 8 * y},
        'z': {'replica': 1 - z},
    }
    return d, c, x, y, z, peers


def neighbour_barrier(peers):
    barrier = pltpu.get_barrier_semaphore()
    for peer in peers:
        pl.semaphore_signal(barrier, inc=1, device_id=peer, device_id_type=MESH)
    pl.semaphore_wait(barrier, len(peers))


def grad_scratch(rows, cols):
    return [pltpu.VMEM((2, 2, 2, rows, cols), F32),
            pltpu.VMEM((2, 2, 2, rows, cols), F32),
            pltpu.VMEM((2, 2, rows, cols), F32),
            pltpu.VMEM((2, 2, rows, cols), F32),
            pltpu.VMEM((2, rows, cols), F32),
            pltpu.VMEM((2, rows, cols), F32),
            pltpu.VMEM((rows, cols), F32),
            pltpu.VMEM((2, rows, cols), F32),
            pltpu.SemaphoreType.DMA((4, 2)),
            pltpu.SemaphoreType.DMA((4, 2))]


class Reducer:
    def __init__(self, scratch, x_first, t):
        (self.tile, self.in_core, self.chip, self.in_one, self.two, self.in_two, self.four, self.in_rep,
         self.send, self.recv) = scratch
        self.x_first = x_first
        self.t = t
        _, self.c, self.x, self.y, _, self.peers = coordinates()

    def copy(self, stage, tile_index):
        slot = lax.rem(tile_index + 2, 2)
        first, second = ('x', 'y') if self.x_first else ('y', 'x')
        if stage == 0:
            src, dst, peer = self.tile.at[:, :, 1 - self.c], self.in_core.at[slot], 'c'
        elif stage == 1:
            src = self.chip.at[:, 1 - self.x] if self.x_first else self.chip.at[1 - self.y]
            dst, peer = self.in_one.at[slot], first
        elif stage == 2:
            src = self.two.at[1 - self.y] if self.x_first else self.two.at[1 - self.x]
            dst, peer = self.in_two.at[slot], second
        else:
            src, dst, peer = self.four, self.in_rep.at[slot], 'z'
        return pltpu.make_async_remote_copy(
            src_ref=src, dst_ref=dst, send_sem=self.send.at[stage, slot], recv_sem=self.recv.at[stage, slot],
            device_id=self.peers[peer], device_id_type=MESH)

    def start(self):
        self.copy(0, self.t).start()

    def progress(self, out_ref, sq_ref):
        t = self.t

        @pl.when(t >= 4)
        def _():
            self.copy(3, t - 4).wait()
            total = self.four[...] + self.in_rep[lax.rem(t, 2)]
            out_ref[0] = total
            sq_ref[...] += jnp.sum(total * total, axis=0, keepdims=True)

        @pl.when((t >= 3) & (t < NT + 3))
        def _():
            self.copy(2, t - 3).wait()
            mine = self.two[self.y] if self.x_first else self.two[self.x]
            self.four[...] = mine + self.in_two[lax.rem(t + 1, 2)]
            self.copy(3, t - 3).start()

        @pl.when((t >= 2) & (t < NT + 2))
        def _():
            self.copy(1, t - 2).wait()
            mine = self.chip[:, self.x] if self.x_first else self.chip[self.y]
            self.two[...] = mine + self.in_one[lax.rem(t, 2)]
            self.copy(2, t - 2).start()

        @pl.when((t >= 1) & (t < NT + 1))
        def _():
            self.copy(0, t - 1).wait()
            self.chip[...] = self.tile[:, :, self.c] + self.in_core[lax.rem(t + 1, 2)]
            self.copy(1, t - 1).start()


def permute_kernel(w_ref, out_ref):
    for t in range(NT):
        out_ref[:, t * TILE:(t + 1) * TILE] = jnp.concatenate(
            [w_ref[:, d * (FF // OWN) + t * PIECE:d * (FF // OWN) + (t + 1) * PIECE] for d in range(OWN)], axis=1)


def permute_columns(w_up):
    rows = 128
    flat = w_up.reshape(2 * D, FF)
    out = pl.pallas_call(
        permute_kernel,
        grid=(2 * D // rows,),
        in_specs=[pl.BlockSpec((rows, FF), lambda i: (i, 0))],
        out_specs=pl.BlockSpec((rows, FF), lambda i: (i, 0)),
        out_shape=jax.ShapeDtypeStruct((2 * D, FF), w_up.dtype),
        name="permute_columns",
    )(flat)
    return out.reshape(2, D, FF)


def forward_kernel(x_ref, wu_ref, wd_ref, z_ref, h_ref, acc):
    t = pl.program_id(0)

    @pl.when(t == 0)
    def _():
        acc[...] = jnp.zeros_like(acc)

    wd = wd_ref[0, :, 0].reshape(TILE, D)

    for r in range(NB + 1):
        if r < NB:
            rows = pl.ds(r * RM, RM)
            z_ref[0, rows, :] = mm(x_ref[rows, :], wu_ref[0]).astype(BF16)
        if r > 0:
            rows = pl.ds((r - 1) * RM, RM)
            u = gelu_value(z_ref[0, rows, :].astype(F32)).astype(BF16)
            acc[rows, :] += mm(u, wd)

    @pl.when(t == NT - 1)
    def _():
        h_ref[...] = acc[...].astype(BF16)


def forward(x, w_upp, w_down5):
    return pl.pallas_call(
        forward_kernel,
        grid=(NT,),
        in_specs=[
            pl.BlockSpec((ROWS, D), lambda t: (0, 0), pipeline_mode=pl.Buffered(1)),
            pl.BlockSpec((1, D, TILE), lambda t: (0, 0, t)),
            pl.BlockSpec((1, OWN, 1, PIECE, D), lambda t: (0, 0, t, 0, 0)),
        ],
        out_specs=[
            pl.BlockSpec((1, ROWS, TILE), lambda t: (t, 0, 0)),
            pl.BlockSpec((ROWS, D), lambda t: (0, 0), pipeline_mode=pl.Buffered(1)),
        ],
        out_shape=[jax.ShapeDtypeStruct((NT, ROWS, TILE), BF16), jax.ShapeDtypeStruct((ROWS, D), BF16)],
        scratch_shapes=[pltpu.VMEM((ROWS, D), F32)],
        compiler_params=pltpu.CompilerParams(vmem_limit_bytes=VMEM_LIMIT),
        name="forward",
    )(x, w_upp, w_down5)


def upper_kernel(h_hbm, ht_hbm, dy_hbm, dyt_hbm, wu_ref, wd_ref, gd_ref, gu_ref, sqd_ref, squ_ref, dh_hbm, dht_hbm,
                 h, ht, dy, dyt, acc, u_s, d_s, sems, *grads):
    t = pl.program_id(0)
    loads = [pltpu.make_async_copy(s, v, sems.at[i]) for i, (s, v) in
             enumerate([(h_hbm, h), (dy_hbm, dy), (dyt_hbm, dyt), (ht_hbm, ht)])]
    stores = [pltpu.make_async_copy(h, dh_hbm, sems.at[0]), pltpu.make_async_copy(ht, dht_hbm, sems.at[1])]
    down = Reducer(grads[:10], True, t)
    up = Reducer(grads[10:], False, t)

    @pl.when(t == 0)
    def _():
        for copy in loads:
            copy.start()
        neighbour_barrier([down.peers[k] for k in 'cxyz'])
        acc[...] = jnp.zeros_like(acc)
        sqd_ref[...] = jnp.zeros_like(sqd_ref)
        squ_ref[...] = jnp.zeros_like(squ_ref)
        loads[0].wait()
        loads[1].wait()

    def rows_of(first, last):
        wu = wu_ref[0]
        wd = wd_ref[0, :, 0].reshape(TILE, D)
        for r in range(first, last):
            if r < NB:
                rows = pl.ds(r * RM, RM)
                u_s[rows, :] = mm(h[rows, :], wu).astype(BF16)
                d_s[rows, :] = mm_nt(dy[rows, :], wd).astype(BF16)
            if r > 0:
                rows = pl.ds((r - 1) * RM, RM)
                u, slope = gelu_both(u_s[rows, :].astype(F32))
                dz = (d_s[rows, :].astype(F32) * slope).astype(BF16)
                u_s[rows, :] = u.astype(BF16)
                d_s[rows, :] = dz
                acc[rows, :] += mm_nt(dz, wu)

    @pl.when(t < NT)
    def _():
        rows_of(0, NB // 2)

    down.progress(gd_ref, sqd_ref)

    @pl.when(t < NT)
    def _():
        rows_of(NB // 2, NB + 1)

    up.progress(gu_ref, squ_ref)

    @pl.when(t == 0)
    def _():
        loads[2].wait()
        loads[3].wait()

    @pl.when(t < NT)
    def _():
        down.tile[...] = mm(dyt[...], u_s[...]).T.reshape(2, 2, 2, PIECE, D)
        up.tile[...] = mm(ht[...], d_s[...]).reshape(2, 2, 2, D // OWN, TILE)
        down.start()
        up.start()

    @pl.when(t == NT - 1)
    def _():
        h[...] = acc[...].astype(BF16)
        stores[0].start()

    @pl.when(t == NT)
    def _():
        ht[...] = h[...].T
        stores[1].start()

    @pl.when(t == GRID - 1)
    def _():
        stores[0].wait()
        stores[1].wait()


def final_tile(t):
    return jnp.clip(t - LAG, 0, NT - 1)


def this_tile(t):
    return jnp.minimum(t, NT - 1)


GRAD_SPECS = [
    pl.BlockSpec((1, PIECE, D), lambda t: (final_tile(t), 0, 0)),
    pl.BlockSpec((1, D // OWN, TILE), lambda t: (final_tile(t), 0, 0)),
    pl.BlockSpec((1, D), lambda t: (0, 0)),
    pl.BlockSpec((1, TILE), lambda t: (0, 0)),
]
GRAD_SHAPES = [
    jax.ShapeDtypeStruct((NT, PIECE, D), F32),
    jax.ShapeDtypeStruct((NT, D // OWN, TILE), F32),
    jax.ShapeDtypeStruct((1, D), F32),
    jax.ShapeDtypeStruct((1, TILE), F32),
]


def upper(h, ht, dy, dyt, w_upp, w_down5):
    anyspec = pl.BlockSpec(memory_space=pl.ANY)
    return pl.pallas_call(
        upper_kernel,
        grid=(GRID,),
        in_specs=[anyspec] * 4 + [
            pl.BlockSpec((1, D, TILE), lambda t: (1, 0, this_tile(t))),
            pl.BlockSpec((1, OWN, 1, PIECE, D), lambda t: (1, 0, this_tile(t), 0, 0)),
        ],
        out_specs=GRAD_SPECS + [anyspec, anyspec],
        out_shape=GRAD_SHAPES + [jax.ShapeDtypeStruct((ROWS, D), BF16), jax.ShapeDtypeStruct((D, ROWS), BF16)],
        scratch_shapes=[pltpu.VMEM((ROWS, D), BF16), pltpu.VMEM((D, ROWS), BF16),
                        pltpu.VMEM((ROWS, D), BF16), pltpu.VMEM((D, ROWS), BF16),
                        pltpu.VMEM((ROWS, D), F32), pltpu.VMEM((ROWS, TILE), BF16), pltpu.VMEM((ROWS, TILE), BF16),
                        pltpu.SemaphoreType.DMA((4,))] + grad_scratch(PIECE, D) + grad_scratch(D // OWN, TILE),
        compiler_params=pltpu.CompilerParams(vmem_limit_bytes=VMEM_LIMIT, collective_id=0, has_side_effects=True),
        name="upper",
    )(h, ht, dy, dyt, w_upp, w_down5)


def lower_kernel(sqd_in, squ_in, dh_hbm, dht_hbm, xt_hbm, z_ref, wd_ref, gd_ref, gu_ref, sqd_ref, squ_ref, norm_ref,
                 dh, dht, xt, u_s, d_s, sems, sq_mine, sq_all, sq_send, sq_recv, *grads):
    t = pl.program_id(0)
    loads = [pltpu.make_async_copy(s, v, sems.at[i]) for i, (s, v) in
             enumerate([(dh_hbm, dh), (dht_hbm, dht), (xt_hbm, xt)])]
    down = Reducer(grads[:10], True, t)
    up = Reducer(grads[10:], False, t)
    me = lax.axis_index('data')
    others = [{'data': lax.rem(me + k, OWN)} for k in range(1, OWN)]

    @pl.when(t == 0)
    def _():
        for copy in loads:
            copy.start()
        neighbour_barrier(others + [down.peers['z']])
        sqd_ref[...] = sqd_in[...]
        squ_ref[...] = squ_in[...]
        loads[0].wait()

    def rows_of(first, last):
        wd = wd_ref[0, :, 0].reshape(TILE, D)
        for r in range(first, last):
            if r < NB:
                rows = pl.ds(r * RM, RM)
                d_s[rows, :] = mm_nt(dh[rows, :], wd).astype(BF16)
            if r > 0:
                rows = pl.ds((r - 1) * RM, RM)
                u, slope = gelu_both(z_ref[0, rows, :].astype(F32))
                u_s[rows, :] = u.astype(BF16)
                d_s[rows, :] = (d_s[rows, :].astype(F32) * slope).astype(BF16)

    @pl.when(t < NT)
    def _():
        rows_of(0, NB // 2)

    down.progress(gd_ref, sqd_ref)

    @pl.when(t < NT)
    def _():
        rows_of(NB // 2, NB + 1)

    up.progress(gu_ref, squ_ref)

    @pl.when(t == 0)
    def _():
        loads[1].wait()
        loads[2].wait()

    @pl.when(t < NT)
    def _():
        down.tile[...] = mm(dht[...], u_s[...]).T.reshape(2, 2, 2, PIECE, D)
        up.tile[...] = mm(xt[...], d_s[...]).reshape(2, 2, 2, D // OWN, TILE)
        down.start()
        up.start()

    @pl.when(t == GRID - 1)
    def _():
        part = jnp.sum(sqd_ref[...], axis=1, keepdims=True) + jnp.sum(squ_ref[...], axis=1, keepdims=True)
        sq_mine[...] = jnp.broadcast_to(part, sq_mine.shape)
        sq_all[me] = sq_mine[...]
        copies = [pltpu.make_async_remote_copy(
            src_ref=sq_mine, dst_ref=sq_all.at[me], send_sem=sq_send.at[k], recv_sem=sq_recv.at[k],
            device_id=others[k], device_id_type=MESH) for k in range(OWN - 1)]
        for copy in copies:
            copy.start()
        for copy in copies:
            copy.wait()
        total = sq_all[0]
        for k in range(1, OWN):
            total = total + sq_all[k]
        norm_ref[...] = total


def lower(sqd, squ, dh, dht, xt, z, w_down5):
    anyspec = pl.BlockSpec(memory_space=pl.ANY)
    return pl.pallas_call(
        lower_kernel,
        grid=(GRID,),
        in_specs=GRAD_SPECS[2:] + [anyspec] * 3 + [
            pl.BlockSpec((1, ROWS, TILE), lambda t: (this_tile(t), 0, 0)),
            pl.BlockSpec((1, OWN, 1, PIECE, D), lambda t: (0, 0, this_tile(t), 0, 0)),
        ],
        out_specs=GRAD_SPECS + [pl.BlockSpec((8, 128), lambda t: (0, 0))],
        out_shape=GRAD_SHAPES + [jax.ShapeDtypeStruct((8, 128), F32)],
        scratch_shapes=[pltpu.VMEM((ROWS, D), BF16), pltpu.VMEM((D, ROWS), BF16), pltpu.VMEM((D, ROWS), BF16),
                        pltpu.VMEM((ROWS, TILE), BF16), pltpu.VMEM((ROWS, TILE), BF16),
                        pltpu.SemaphoreType.DMA((3,)),
                        pltpu.VMEM((8, 128), F32), pltpu.VMEM((OWN, 8, 128), F32),
                        pltpu.SemaphoreType.DMA((OWN - 1,)), pltpu.SemaphoreType.DMA((OWN - 1,))]
        + grad_scratch(PIECE, D) + grad_scratch(D // OWN, TILE),
        compiler_params=pltpu.CompilerParams(vmem_limit_bytes=VMEM_LIMIT, collective_id=1, has_side_effects=True),
        name="lower",
    )(sqd, squ, dh, dht, xt, z, w_down5)


def adam_update(grad_vals, master_vals, mom_vals, var_vals, clip_scale):
    new_mom = BETA1 * mom_vals + (1.0 - BETA1) * clip_scale * grad_vals
    new_var = BETA2 * var_vals + (1.0 - BETA2) * (clip_scale * clip_scale) * (grad_vals * grad_vals)
    new_master = master_vals - LEARN_RATE * (new_mom / BIAS_ONE) / (jnp.sqrt(new_var / BIAS_TWO) + ADAM_EPS)
    return new_master, new_mom, new_var


def unpermute(shard):
    rows = shard.shape[1]
    return shard.reshape(NT, rows, OWN, PIECE).transpose(1, 2, 0, 3).reshape(rows, FF)


def solution(mesh):
    total_devices = mesh.shape['replica'] * mesh.shape['data']
    batch_spec = P(('replica', 'data'), None)
    whole_spec = P()
    shard_spec = P(None, 'data', None)

    def device_step(inp_rows, out_grad, w_up, w_down, master_up, master_down, mom_up, mom_down, var_up, var_down, clip_norm):
        w_upp = permute_columns(w_up)
        w_down5 = w_down.reshape(2, OWN, NT, PIECE, D)
        pre_one, mid_rows = forward(inp_rows, w_upp, w_down5)
        shard_down2, shard_up2, sqd, squ, dmid_rows, dmid_t = upper(
            mid_rows, mid_rows.T, out_grad, out_grad.T, w_upp, w_down5)
        shard_down1, shard_up1, _, _, square_sum = lower(
            sqd, squ, dmid_rows, dmid_t, inp_rows.T, pre_one, w_down5)
        grad_up = jnp.stack([unpermute(shard_up1), unpermute(shard_up2)]) / total_devices
        grad_down = jnp.stack([shard_down1.reshape(FF // OWN, D), shard_down2.reshape(FF // OWN, D)]) / total_devices
        grad_norm = jnp.sqrt(square_sum[0, 0]) / total_devices
        clip_scale = jnp.minimum(1.0, clip_norm / (grad_norm + NORM_EPS))
        master_up_new, mom_up_new, var_up_new = adam_update(grad_up, master_up, mom_up, var_up, clip_scale)
        master_down_new, mom_down_new, var_down_new = adam_update(grad_down, master_down, mom_down, var_down, clip_scale)
        w_up_new = lax.all_gather(master_up_new.astype(jnp.bfloat16), 'data', axis=1, tiled=True)
        w_down_new = lax.all_gather(master_down_new.astype(jnp.bfloat16), 'data', axis=1, tiled=True)
        return (w_up_new, w_down_new, master_up_new, master_down_new, mom_up_new, mom_down_new, var_up_new, var_down_new, grad_norm)

    return jax.shard_map(device_step, mesh=mesh, in_specs=(batch_spec, batch_spec, whole_spec, whole_spec, shard_spec, shard_spec, shard_spec, shard_spec, shard_spec, shard_spec, whole_spec), out_specs=(whole_spec, whole_spec, shard_spec, shard_spec, shard_spec, shard_spec, shard_spec, shard_spec, whole_spec), check_vma=False)
```

time: 1480 us -> 846 us (0.57)
  waiting for transfers between devices: 672 us -> 119 us
  Pallas kernels: 617 us -> 576 us
  other arithmetic: 39.4 us -> 22 us
  local copies, waits for them, and re-layouts: 121 us -> 104 us
    reduce_scatter x4 -> x0, waiting for transfers between devices: 336 us -> none  [the longest x1 117 us: device_step(): lax.psum_scatter(grad_down1, 'data', scatter_dimension=0, tiled=True)]
    psum x1 -> x0, waiting for transfers between devices: 203 us -> none  [device_step(): lax.psum(jnp.stack([shard_up1, shard_up2]), 'replica') / total_devices]
    pallas_call x1, Pallas kernels: 180 us -> 96.1 us  [forward(): pl.pallas_call(forward_kernel, grid=(NT,), in_specs=[pl.BlockSpec((ROWS,...]
    all_gather x1, waiting for transfers between devices: 75 us -> 28.2 us  [device_step(): lax.all_gather(master_down_new.astype(jnp.bfloat16), 'data', axis=1, tile...]
    pallas_call x2, Pallas kernels: 415 us -> 458 us  [the longest x1 269 us: upper(): pl.pallas_call(upper_kernel, grid=(GRID,), in_specs=[anyspec] * 4 + [pl.B...]
    all_gather x1, waiting for transfers between devices: 57.4 us -> 90.5 us  [device_step(): lax.all_gather(master_up_new.astype(jnp.bfloat16), 'data', axis=1, tiled=...]
    unnamed x12 -> x14, local copies, waits for them, and re-layouts: 84.9 us -> 78.2 us
  transfers between devices with their start and end apart: 7 -> 2, of which waited for: 6 -> 2; matrix products, arithmetic and copies ran while one was open for 6% -> 7% of each run, Pallas kernels for 11% -> 0%
where the time goes in v2:
time: 846 us; the launch traced here: 838 us
  Pallas kernels  576 us (68%)
  waiting for transfers between devices  119 us (14%)
  local copies, waits for them, and re-layouts  104 us (12%)
  other arithmetic  22 us (3%)
  between operations  17 us (2%)
    pallas_call x1, Pallas kernels, upper(): pl.pallas_call(upper_kernel, grid=(GRID,), in_specs=[anyspec] * 4 + [pl.B...  269 us
    pallas_call x1, Pallas kernels, lower(): pl.pallas_call(lower_kernel, grid=(GRID,), in_specs=GRAD_SPECS[2:] + [any...  189 us
    pallas_call x1, Pallas kernels, forward(): pl.pallas_call(forward_kernel, grid=(NT,), in_specs=[pl.BlockSpec((ROWS,...  96.1 us
    all_gather x1, waiting for transfers between devices, device_step(): lax.all_gather(master_up_new.astype(jnp.bfloat16), 'data', axis=1, tiled=...  90.5 us
    unnamed x14, local copies, waits for them, and re-layouts  78.2 us
    all_gather x1, waiting for transfers between devices, device_step(): lax.all_gather(master_down_new.astype(jnp.bfloat16), 'data', axis=1, tile...  28.2 us
    pallas_call x1, Pallas kernels, permute_columns(): pl.pallas_call(permute_kernel, grid=(2 * D // rows,), in_specs=[pl.BlockS...  21.5 us
  transfers between devices with their start and end apart: 2, of which 2 were waited for; matrix products, arithmetic and copies ran while one was open for 7% of the time, Pallas kernels for 0%

profile of v2, /device:TPU:0, one launch (start us, length us, event | category | flops | bytes accessed | tf_op | source)
XLA Modules:
  0.0 837.8 jit_solution(1023532317019723621)
XLA Ops:
  7.2 0.0 all-gather.5.cloned.1.call-start
  7.2 21.5 %permute_columns.1 = bf16[1792,4864]{1,0:T(8,128)(2,1)} custom-call(bf16[1792,4864]{1,0:T(8,128)(2,1)} %bitcast.25), custom_call_target="tpu_custom_call" | custom-call | tf_op jit(solution)/shard_map/permute_columns/pallas_call | solution.py:158
  28.7 10.7 %copy.42 = bf16[4096,896]{0,1:T(8,128)(2,1)} copy(bf16[4096,896]{1,0:T(8,128)(2,1)} %x_ref.1) | data formatting | bytes 14680064 | tf_op args[0]
  39.5 96.1 %forward.1 = (bf16[19,4096,256]{2,1,0:T(8,128)(2,1)}, bf16[4096,896]{1,0:T(8,128)(2,1)}) custom-call(bf16[4096,896]{1,0:T(8,128)(2,1)} %x_ref.1, bf16[2,896,4864]{2,1,0:T(8,128)(2,1)} %bitcast.17, bf16[2,8,19,32,896]{4,3,2,1,0:T(8,128)(2,1)} %bitcast.19), custom_call_target="tpu_custom_call" | custom-call | tf_op jit(solution)/shard_map/forward/pallas_call | solution.py:193
  135.6 10.8 %copy.40 = bf16[4096,896]{0,1:T(8,128)(2,1)} copy(bf16[4096,896]{1,0:T(8,128)(2,1)} %get-tuple-element.20.h_hbm) | data formatting | bytes 14680064 | tf_op jit(solution)/shard_map/forward/pallas_call | solution.py:193
  146.3 10.7 %copy.41 = bf16[4096,896]{0,1:T(8,128)(2,1)} copy(bf16[4096,896]{1,0:T(8,128)(2,1)} %dy_hbm.1) | data formatting | bytes 14680064 | tf_op args[1]
  157.0 269.2 %upper.1 = (f32[19,32,896]{2,1,0:T(8,128)}, f32[19,112,256]{2,1,0:T(8,128)}, f32[1,896]{1,0:T(1,128)}, f32[1,256]{1,0:T(1,128)}, bf16[4096,896]{1,0:T(8,128)(2,1)}, /*index=5*/bf16[896,4096]{1,0:T(8,128)(2,1)}) custom-call(bf16[4096,896]{1,0:T(8,128)(2,1)} %get-tuple-element.20.h_hbm, bf16[896,4096]{1,0:T(8,128)(2,1)} %bitcast.23, bf16[4096,896]{1,0:T(8,128)(2,1)} %dy_hbm.1, ...), custom_call_target="tpu_custom_call" | custom-call | tf_op jit(solution)/shard_map/upper/pallas_call | solution.py:312
  426.2 188.8 %lower.1 = (f32[19,32,896]{2,1,0:T(8,128)}, f32[19,112,256]{2,1,0:T(8,128)}, f32[1,896]{1,0:T(1,128)}, f32[1,256]{1,0:T(1,128)}, f32[8,128]{1,0:T(8,128)}) custom-call(f32[1,896]{1,0:T(1,128)} %get-tuple-element.21.sqd_in, f32[1,256]{1,0:T(1,128)} %get-tuple-element.22.squ_in, bf16[4096,896]{1,0:T(8,128)(2,1)} %get-tuple-element.23.dh_hbm, ...), custom_call_target="tpu_custom_call" | custom-call | tf_op jit(solution)/shard_map/lower/pallas_call | solution.py:405
  614.9 1.2 slice.3
  617.5 10.5 %fusion = (bf16[2,608,896]{2,1,0:T(8,128)(2,1)}, f32[2,608,896]{2,1,0:T(8,128)}, f32[2,608,896]{2,1,0:T(8,128)}, f32[2,608,896]{2,1,0:T(8,128)}) fusion(f32[2,608,896]{2,1,0:T(8,128)} %param.16, f32[]{:T(128)S(6)} %mul.80, f32[1,608,896]{2,1,0:T(8,128)} %bitcast.30, f32[1,608,896]{2,1,0:T(8,128)} %bitcast.31, f32[2,608,896]{2,1,0:T(8,128)} %param.18, ...), kind=kLoop, calls=%fused_computation.8 | loop fusion | flops 16343040 | bytes 32686088 | tf_op jit(solution)/shard_map/convert_element_type | solution.py:458
  628.1 0.0 all-gather.5.cloned.1.call-update
  628.1 0.0 all-gather.3.cloned.1.call-start
  628.1 2.3 copy.43
  630.5 1.7 copy.44
  632.2 2.1 copy.45
  634.2 1.7 copy.46
  635.9 5.6 copy.39
  641.6 5.6 copy.47
  647.2 0.0 copy-start.1
  647.2 5.8 copy.48
  652.9 0.0 copy-done.1
  652.9 11.5 %fusion.1 = (bf16[2,112,4864]{1,2,0:T(8,128)(2,1)}, f32[2,112,4864]{1,2,0:T(8,128)}, f32[2,112,4864]{1,2,0:T(8,128)}, f32[2,112,4864]{1,2,0:T(8,128)}) fusion(f32[2,112,4864]{1,2,0:T(8,128)} %copy.48, f32[]{:T(128)S(6)} %mul.80, f32[1,112,4864]{1,2,0:T(8,128)} %bitcast.29, f32[1,112,4864]{1,2,0:T(8,128)S(1)} %bitcast.28, f32[2,112,4864]{1,2,0:T(8,128)} %copy.39, ...), kind=kLoop, calls=%fused_computation.9 | loop fusion | flops 16343040 | bytes 32686088 | tf_op jit(solution)/shard_map/convert_element_type | solution.py:457
  664.4 6.4 copy.49
  670.8 0.0 all-gather.3.cloned.1.call-update
  670.8 5.6 copy.51
  676.4 5.6 copy.52
  682.0 5.6 copy.53
  687.6 28.2 %all-gather.5.cloned.1.call-done = bf16[2,4864,896]{2,1,0:T(8,128)(2,1)} async-done(((bf16[2,608,896]{2,1,0:T(8,128)(2,1)}), bf16[2,4864,896]{2,1,0:T(8,128)(2,1)}) %all-gather.5.cloned.1.call-update) | async-done | bytes 17432592 | tf_op jit(solution)/shard_map/all_gather | solution.py:458
  715.8 90.5 %all-gather.3.cloned.1.call-done = bf16[2,896,4864]{2,0,1:T(2,128)(2,1)} async-done(((bf16[2,112,4864]{2,0,1:T(2,128)(2,1)}), bf16[2,896,4864]{2,0,1:T(2,128)(2,1)}) %all-gather.3.cloned.1.call-update) | async-done | bytes 17432592 | tf_op jit(solution)/shard_map/all_gather | solution.py:457
  806.4 16.7 %copy.50 = bf16[2,896,4864]{2,1,0:T(8,128)(2,1)} copy(bf16[2,896,4864]{2,0,1:T(2,128)(2,1)} %all-gather.3.cloned.1.call-done) | data formatting | bytes 34865152
  823.0 0.0 copy-done
  823.0 6.4 copy.56
  (1 shorter events, 0.0 us)
Async XLA Ops:
  7.2 708.6 %all-gather.5.cloned.1.call-start = ((), (), s32[]{:S(2)}) async-start(), calls=%async_computation.1 | async-start | bytes 19611648 | tf_op jit(solution)/shard_map/all_gather | solution.py:458
  628.1 178.3 %all-gather.3.cloned.1.call-start = ((), (), s32[]{:S(2)}) async-start(), calls=%async_computation | async-start | bytes 19611648 | tf_op jit(solution)/shard_map/all_gather | solution.py:457
  647.2 5.8 copy-start.1
  806.3 16.7 %copy-start = (bf16[2,4864,896]{2,1,0:T(8,128)(2,1)S(1)}, bf16[2,4864,896]{2,1,0:T(8,128)(2,1)}, u32[]{:S(2)}) copy-start(bf16[2,4864,896]{2,1,0:T(8,128)(2,1)} %all-gather.5.cloned.1.call-done) | copy-start | bytes 52297732
Sparse Core Ops, SparseCore 0:
  628.2 87.5 all-gather.4
  717.7 88.6 all-gather.2

commit v3 on v2

--- a/solution.py
+++ b/solution.py
@@ -166,15 +166,15 @@
     return out.reshape(2, D, FF)
 
 
-def forward_kernel(x_ref, wu_ref, wd_ref, z_ref, h_ref, acc):
+def forward_kernel(x_ref, dy_ref, wu_ref, wd_ref, z_ref, h_ref, ht_ref, xt_ref, dyt_ref, acc):
     t = pl.program_id(0)
+    block = jnp.minimum(t, ROWS // TILE - 1)
 
     @pl.when(t == 0)
     def _():
         acc[...] = jnp.zeros_like(acc)
 
     wd = wd_ref[0, :, 0].reshape(TILE, D)
-
     for r in range(NB + 1):
         if r < NB:
             rows = pl.ds(r * RM, RM)
@@ -183,30 +183,43 @@
             rows = pl.ds((r - 1) * RM, RM)
             u = gelu_value(z_ref[0, rows, :].astype(F32)).astype(BF16)
             acc[rows, :] += mm(u, wd)
+        if r == 2:
+            xt_ref[...] = x_ref[pl.ds(pl.multiple_of(block * TILE, TILE), TILE), :].T
+        if r == 5:
+            dyt_ref[...] = dy_ref[...].T
 
     @pl.when(t == NT - 1)
     def _():
         h_ref[...] = acc[...].astype(BF16)
-
-
-def forward(x, w_upp, w_down5):
+        ht_ref[...] = h_ref[...].T
+
+
+def forward(x, dy, w_upp, w_down5):
+    last = ROWS // TILE - 1
+    once = pl.Buffered(1)
     return pl.pallas_call(
         forward_kernel,
         grid=(NT,),
         in_specs=[
-            pl.BlockSpec((ROWS, D), lambda t: (0, 0), pipeline_mode=pl.Buffered(1)),
+            pl.BlockSpec((ROWS, D), lambda t: (0, 0), pipeline_mode=once),
+            pl.BlockSpec((TILE, D), lambda t: (jnp.minimum(t, last), 0)),
             pl.BlockSpec((1, D, TILE), lambda t: (0, 0, t)),
             pl.BlockSpec((1, OWN, 1, PIECE, D), lambda t: (0, 0, t, 0, 0)),
         ],
         out_specs=[
             pl.BlockSpec((1, ROWS, TILE), lambda t: (t, 0, 0)),
-            pl.BlockSpec((ROWS, D), lambda t: (0, 0), pipeline_mode=pl.Buffered(1)),
+            pl.BlockSpec((ROWS, D), lambda t: (0, 0), pipeline_mode=once),
+            pl.BlockSpec((D, ROWS), lambda t: (0, 0), pipeline_mode=once),
+            pl.BlockSpec((D, TILE), lambda t: (0, jnp.minimum(t, last))),
+            pl.BlockSpec((D, TILE), lambda t: (0, jnp.minimum(t, last))),
         ],
-        out_shape=[jax.ShapeDtypeStruct((NT, ROWS, TILE), BF16), jax.ShapeDtypeStruct((ROWS, D), BF16)],
+        out_shape=[jax.ShapeDtypeStruct((NT, ROWS, TILE), BF16), jax.ShapeDtypeStruct((ROWS, D), BF16),
+                   jax.ShapeDtypeStruct((D, ROWS), BF16), jax.ShapeDtypeStruct((D, ROWS), BF16),
+                   jax.ShapeDtypeStruct((D, ROWS), BF16)],
         scratch_shapes=[pltpu.VMEM((ROWS, D), F32)],
         compiler_params=pltpu.CompilerParams(vmem_limit_bytes=VMEM_LIMIT),
         name="forward",
-    )(x, w_upp, w_down5)
+    )(x, dy, w_upp, w_down5)
 
 
 def upper_kernel(h_hbm, ht_hbm, dy_hbm, dyt_hbm, wu_ref, wd_ref, gd_ref, gu_ref, sqd_ref, squ_ref, dh_hbm, dht_hbm,
@@ -429,13 +442,190 @@
     return new_master, new_mom, new_var
 
 
-def unpermute(shard):
-    rows = shard.shape[1]
-    return shard.reshape(NT, rows, OWN, PIECE).transpose(1, 2, 0, 3).reshape(rows, FF)
+def norm_and_clip(sq_ref, clip_ref):
+    norm = jnp.sqrt(sq_ref[...]) / DEVICES
+    return norm, jnp.minimum(1.0, clip_ref[0, 0] / (norm + NORM_EPS))[0:1, 0:1]
+
+
+UP_ROWS = D // OWN
+DOWN_ROWS = FF // OWN
+DEVICES = 16
+
+
+def adam_up_kernel(sq_ref, clip_ref, one_ref, two_ref, master_ref, mom_ref, var_ref,
+                   new_w_ref, new_master_ref, new_mom_ref, new_var_ref):
+    _, scale = norm_and_clip(sq_ref, clip_ref)
+
+    def update(g_ref):
+        for n in range(FF // 128):
+            pieces = [divmod(4 * n + q, NT) for q in range(4)]
+            grad = jnp.concatenate([g_ref[t, :, d * PIECE:(d + 1) * PIECE] for d, t in pieces], axis=1) / DEVICES
+            cols = pl.ds(n * 128, 128)
+            master, mom, var = adam_update(grad, master_ref[0, :, cols], mom_ref[0, :, cols], var_ref[0, :, cols], scale)
+            new_master_ref[0, :, cols] = master
+            new_mom_ref[0, :, cols] = mom
+            new_var_ref[0, :, cols] = var
+            new_w_ref[0, :, cols] = master.astype(BF16)
+
+    pl.when(pl.program_id(0) == 0)(lambda: update(one_ref))
+    pl.when(pl.program_id(0) == 1)(lambda: update(two_ref))
+
+
+def adam_down_kernel(sq_ref, clip_ref, one_ref, two_ref, master_ref, mom_ref, var_ref,
+                     new_w_ref, new_master_ref, new_mom_ref, new_var_ref, norm_ref):
+    norm, scale = norm_and_clip(sq_ref, clip_ref)
+    norm_ref[...] = norm
+
+    def update(g_ref):
+        def body(i, carry):
+            rows = pl.ds(pl.multiple_of(i * 16, 16), 16)
+            master, mom, var = adam_update(g_ref[rows, :] / DEVICES, master_ref[0, rows, :], mom_ref[0, rows, :],
+                                           var_ref[0, rows, :], scale)
+            new_master_ref[0, rows, :] = master
+            new_mom_ref[0, rows, :] = mom
+            new_var_ref[0, rows, :] = var
+            new_w_ref[0, rows, :] = master.astype(BF16)
+            return carry
+
+        lax.fori_loop(0, g_ref.shape[0] // 16, body, 0)
+
+    pl.when(pl.program_id(0) == 0)(lambda: update(one_ref))
+    pl.when(pl.program_id(0) == 1)(lambda: update(two_ref))
+
+
+def adam_call(kernel, name, square_sum, clip, g_one, g_two, master, mom, var, block, g_block, with_norm):
+    layers, rows, cols = master.shape
+    steps = rows // block
+    dims = len(g_block)
+
+    def state_index(layer, i):
+        return (layer, i, 0)
+
+    def g_index(which):
+        def index(layer, i):
+            fixed = jnp.where(layer == which, i, steps - 1 if which == 0 else 0)
+            return (0, fixed, 0) if dims == 3 else (fixed, 0)
+        return index
+
+    state = pl.BlockSpec((1, block, cols), state_index)
+    small = pl.BlockSpec((8, 128), lambda layer, i: (0, 0))
+    out_specs = [state] * 4 + ([small] if with_norm else [])
+    out_shape = [jax.ShapeDtypeStruct(master.shape, BF16)] + [jax.ShapeDtypeStruct(master.shape, F32)] * 3
+    if with_norm:
+        out_shape = out_shape + [jax.ShapeDtypeStruct((8, 128), F32)]
+    return pl.pallas_call(
+        kernel,
+        grid=(layers, steps),
+        in_specs=[small, pl.BlockSpec(memory_space=pltpu.SMEM),
+                  pl.BlockSpec(g_block, g_index(0)), pl.BlockSpec(g_block, g_index(1)), state, state, state],
+        out_specs=out_specs,
+        out_shape=out_shape,
+        compiler_params=pltpu.CompilerParams(vmem_limit_bytes=VMEM_LIMIT),
+        name=name,
+    )(square_sum, clip, g_one, g_two, master, mom, var)
+
+
+UP_CHUNKS = [(True, 0, 16), (True, 16, 32), (True, 48, 32), (True, 80, 32)]
+DOWN_CHUNKS = [(False, 0, 144), (False, 144, 144), (False, 288, 160), (False, 448, 160)]
+CHUNKS = UP_CHUNKS + DOWN_CHUNKS
+NC = len(CHUNKS)
+GROUPS = 14
+
+
+def gather_kernel(up_hbm, down_hbm, out_up, out_down, up_v, down_v, send, recv, local):
+    d, c, x, y, z, peers = coordinates()
+    d_x = d + 2 - 4 * x
+    d_y = d + 4 - 8 * y
+    d_xy = d_x + 4 - 8 * y
+    other_core = 1 - 2 * c
+
+    loads = [pltpu.make_async_copy(up_hbm, up_v, local.at[0]), pltpu.make_async_copy(down_hbm, down_v, local.at[1])]
+    for copy in loads:
+        copy.start()
+    neighbour_barrier([peers[k] for k in 'cxyz'])
+    for copy in loads:
+        copy.wait()
+
+    def region(chunk, layer, owner):
+        is_up, first, count = CHUNKS[chunk]
+        out, rows = (out_up, UP_ROWS) if is_up else (out_down, DOWN_ROWS)
+        return out.at[layer, pl.ds(pl.multiple_of(owner * rows + first, 16), count)]
+
+    def mine(chunk, layer):
+        is_up, first, count = CHUNKS[chunk]
+        return (up_v if is_up else down_v).at[layer, pl.ds(first, count)]
+
+    started = []
+
+    def send_chunk(group, chunk, src, layer, owner, peer):
+        copy = pltpu.make_async_remote_copy(
+            src_ref=src, dst_ref=region(chunk, layer, owner), send_sem=send.at[group, chunk],
+            recv_sem=recv.at[group, chunk], device_id=peers[peer], device_id_type=MESH)
+        copy.start()
+        started.append(copy)
+
+    def arrived(group, chunk, layer, owner):
+        pltpu.make_async_remote_copy(
+            src_ref=region(chunk, layer, owner), dst_ref=region(chunk, layer, owner), send_sem=send.at[group, chunk],
+            recv_sem=recv.at[group, chunk], device_id=peers['c'], device_id_type=MESH).wait_recv()
+
+    for k in range(NC):
+        send_chunk(0, k, mine(k, z), z, d, 'x')
+        send_chunk(1, k, mine(k, 1 - z), 1 - z, d, 'y')
+    for k in range(NC):
+        send_chunk(6, k, mine(k, 0), 0, d, 'c')
+        send_chunk(7, k, mine(k, 1), 1, d, 'c')
+    stores = []
+    for layer in range(2):
+        stores.append(pltpu.make_async_copy(up_v.at[layer], out_up.at[layer, pl.ds(pl.multiple_of(d * UP_ROWS, 16), UP_ROWS)], local.at[2 + layer]))
+        stores.append(pltpu.make_async_copy(down_v.at[layer], out_down.at[layer, pl.ds(pl.multiple_of(d * DOWN_ROWS, 16), DOWN_ROWS)], local.at[4 + layer]))
+    for copy in stores:
+        copy.start()
+
+    def second(k):
+        for group, core_group, layer, owner in ((4, 10, 1 - z, d_x), (5, 11, z, d_y), (2, 12, z, d_xy), (3, 13, 1 - z, d_xy)):
+            arrived(group, k, layer, owner)
+            send_chunk(core_group, k, region(k, layer, owner), layer, owner, 'c')
+
+    for k in range(NC):
+        arrived(0, k, z, d_x)
+        src = region(k, z, d_x)
+        send_chunk(4, k, src, z, d_x, 'z')
+        send_chunk(2, k, src, z, d_x, 'y')
+        send_chunk(8, k, src, z, d_x, 'c')
+        arrived(1, k, 1 - z, d_y)
+        src = region(k, 1 - z, d_y)
+        send_chunk(5, k, src, 1 - z, d_y, 'z')
+        send_chunk(3, k, src, 1 - z, d_y, 'x')
+        send_chunk(9, k, src, 1 - z, d_y, 'c')
+    for k in range(NC):
+        second(k)
+    for k in range(NC):
+        for group, layer, owner in ((6, 0, d), (7, 1, d), (8, z, d_x), (9, 1 - z, d_y), (10, 1 - z, d_x),
+                                    (11, z, d_y), (12, z, d_xy), (13, 1 - z, d_xy)):
+            arrived(group, k, layer, owner + other_core)
+    for copy in started:
+        copy.wait_send()
+    for copy in stores:
+        copy.wait()
+
+
+def gather(up_shard, down_shard):
+    anyspec = pl.BlockSpec(memory_space=pl.ANY)
+    return pl.pallas_call(
+        gather_kernel,
+        in_specs=[anyspec, anyspec],
+        out_specs=[anyspec, anyspec],
+        out_shape=[jax.ShapeDtypeStruct((2, D, FF), BF16), jax.ShapeDtypeStruct((2, FF, D), BF16)],
+        scratch_shapes=[pltpu.VMEM((2, UP_ROWS, FF), BF16), pltpu.VMEM((2, DOWN_ROWS, D), BF16),
+                        pltpu.SemaphoreType.DMA((GROUPS, NC)), pltpu.SemaphoreType.DMA((GROUPS, NC)),
+                        pltpu.SemaphoreType.DMA((6,))],
+        compiler_params=pltpu.CompilerParams(vmem_limit_bytes=VMEM_LIMIT, collective_id=2, has_side_effects=True),
+        name="gather",
+    )(up_shard, down_shard)
 
 
 def solution(mesh):
-    total_devices = mesh.shape['replica'] * mesh.shape['data']
     batch_spec = P(('replica', 'data'), None)
     whole_spec = P()
     shard_spec = P(None, 'data', None)
@@ -443,19 +633,17 @@
     def device_step(inp_rows, out_grad, w_up, w_down, master_up, master_down, mom_up, mom_down, var_up, var_down, clip_norm):
         w_upp = permute_columns(w_up)
         w_down5 = w_down.reshape(2, OWN, NT, PIECE, D)
-        pre_one, mid_rows = forward(inp_rows, w_upp, w_down5)
-        shard_down2, shard_up2, sqd, squ, dmid_rows, dmid_t = upper(
-            mid_rows, mid_rows.T, out_grad, out_grad.T, w_upp, w_down5)
-        shard_down1, shard_up1, _, _, square_sum = lower(
-            sqd, squ, dmid_rows, dmid_t, inp_rows.T, pre_one, w_down5)
-        grad_up = jnp.stack([unpermute(shard_up1), unpermute(shard_up2)]) / total_devices
-        grad_down = jnp.stack([shard_down1.reshape(FF // OWN, D), shard_down2.reshape(FF // OWN, D)]) / total_devices
-        grad_norm = jnp.sqrt(square_sum[0, 0]) / total_devices
-        clip_scale = jnp.minimum(1.0, clip_norm / (grad_norm + NORM_EPS))
-        master_up_new, mom_up_new, var_up_new = adam_update(grad_up, master_up, mom_up, var_up, clip_scale)
-        master_down_new, mom_down_new, var_down_new = adam_update(grad_down, master_down, mom_down, var_down, clip_scale)
-        w_up_new = lax.all_gather(master_up_new.astype(jnp.bfloat16), 'data', axis=1, tiled=True)
-        w_down_new = lax.all_gather(master_down_new.astype(jnp.bfloat16), 'data', axis=1, tiled=True)
-        return (w_up_new, w_down_new, master_up_new, master_down_new, mom_up_new, mom_down_new, var_up_new, var_down_new, grad_norm)
+        pre_one, mid_rows, mid_t, inp_t, grad_t = forward(inp_rows, out_grad, w_upp, w_down5)
+        shard_down2, shard_up2, sqd, squ, dmid_rows, dmid_t = upper(mid_rows, mid_t, out_grad, grad_t, w_upp, w_down5)
+        shard_down1, shard_up1, _, _, square_sum = lower(sqd, squ, dmid_rows, dmid_t, inp_t, pre_one, w_down5)
+        clip = clip_norm.reshape(1, 1)
+        w_up_shard, master_up_new, mom_up_new, var_up_new = adam_call(
+            adam_up_kernel, "adam_up", square_sum, clip, shard_up1, shard_up2, master_up, mom_up, var_up,
+            16, (NT, 16, TILE), False)
+        w_down_shard, master_down_new, mom_down_new, var_down_new, norm = adam_call(
+            adam_down_kernel, "adam_down", square_sum, clip, shard_down1.reshape(DOWN_ROWS, D),
+            shard_down2.reshape(DOWN_ROWS, D), master_down, mom_down, var_down, 304, (304, D), True)
+        w_up_new, w_down_new = gather(w_up_shard, w_down_shard)
+        return (w_up_new, w_down_new, master_up_new, master_down_new, mom_up_new, mom_down_new, var_up_new, var_down_new, norm[0, 0])
 
     return jax.shard_map(device_step, mesh=mesh, in_specs=(batch_spec, batch_spec, whole_spec, whole_spec, shard_spec, shard_spec, shard_spec, shard_spec, shard_spec, shard_spec, whole_spec), out_specs=(whole_spec, whole_spec, shard_spec, shard_spec, shard_spec, shard_spec, shard_spec, shard_spec, whole_spec), check_vma=False)

time: 846 us -> 746 us (0.88)
  Pallas kernels: 576 us -> 719 us
  waiting for transfers between devices: 119 us -> 0 us
  local copies, waits for them, and re-layouts: 104 us -> 25.1 us
  other arithmetic: 22 us -> 0 us
  between operations: 17 us -> 1.32 us
    pallas_call x0 -> x3, Pallas kernels: none -> 138 us  [the longest x1 106 us: gather(): pl.pallas_call(gather_kernel, in_specs=[anyspec, anyspec], out_specs=[any...]
    all_gather x2 -> x0, waiting for transfers between devices: 119 us -> none  [the longest x1 90.5 us: device_step(): lax.all_gather(master_up_new.astype(jnp.bfloat16), 'data', axis=1, tiled=...]
    unnamed x14 -> x4, local copies, waits for them, and re-layouts: 78.2 us -> 23.9 us
    convert_element_type x2 -> x0, other arithmetic: 22 us -> none  [the longest x1 11.5 us: device_step(): master_up_new.astype(jnp.bfloat16)]
    pallas_call x3 -> x0, local copies, waits for them, and re-layouts: 15.1 us -> none  [the longest x1 10.8 us: forward(): pl.pallas_call(forward_kernel, grid=(NT,), in_specs=[pl.BlockSpec((ROWS,...]
  transfers between devices with their start and end apart: 2 -> 0, of which waited for: 2 -> 0; matrix products, arithmetic and copies ran while one was open for 7% -> 0% of each run, Pallas kernels for 0% -> 0%
where the time goes in v3:
time: 746 us; the launch traced here: 745 us
  Pallas kernels  719 us (96%)
  local copies, waits for them, and re-layouts  25.1 us (3%)
    pallas_call x1, Pallas kernels, upper(): pl.pallas_call(upper_kernel, grid=(GRID,), in_specs=[anyspec] * 4 + [pl.B...  269 us
    pallas_call x1, Pallas kernels, lower(): pl.pallas_call(lower_kernel, grid=(GRID,), in_specs=GRAD_SPECS[2:] + [any...  189 us
    pallas_call x1, Pallas kernels, gather(): pl.pallas_call(gather_kernel, in_specs=[anyspec, anyspec], out_specs=[any...  106 us
    pallas_call x1, Pallas kernels, forward(): pl.pallas_call(forward_kernel, grid=(NT,), in_specs=[pl.BlockSpec((ROWS,...  101 us
    pallas_call x2, Pallas kernels, adam_call(): pl.pallas_call(kernel, grid=(layers, steps), in_specs=[small, pl.BlockSpe...  31.9 us
    unnamed x4, local copies, waits for them, and re-layouts  23.9 us
    pallas_call x1, Pallas kernels, permute_columns(): pl.pallas_call(permute_kernel, grid=(2 * D // rows,), in_specs=[pl.BlockS...  21.5 us

profile of v3, /device:TPU:0, one launch (start us, length us, event | category | flops | bytes accessed | tf_op | source)
XLA Modules:
  0.0 744.9 jit_solution(8641898574997965329)
XLA Ops:
  0.6 21.5 %permute_columns.1 = bf16[1792,4864]{1,0:T(8,128)(2,1)} custom-call(bf16[1792,4864]{1,0:T(8,128)(2,1)} %bitcast.14), custom_call_target="tpu_custom_call" | custom-call | tf_op jit(solution)/shard_map/permute_columns/pallas_call | solution.py:158
  22.2 101.0 %forward.1 = (bf16[19,4096,256]{2,1,0:T(8,128)(2,1)}, bf16[4096,896]{1,0:T(8,128)(2,1)}, bf16[896,4096]{1,0:T(8,128)(2,1)}, bf16[896,4096]{1,0:T(8,128)(2,1)}, bf16[896,4096]{1,0:T(8,128)(2,1)}) custom-call(bf16[4096,896]{1,0:T(8,128)(2,1)} %x_ref.1, bf16[4096,896]{1,0:T(8,128)(2,1)} %dy_hbm.1, bf16[2,896,4864]{2,1,0:T(8,128)(2,1)} %bitcast.9, ...), custom_call_target="tpu_custom_call" | custom-call | tf_op jit(solution)/shard_map/forward/pallas_call | solution.py:200
  123.2 269.0 %upper.1 = (f32[19,32,896]{2,1,0:T(8,128)}, f32[19,112,256]{2,1,0:T(8,128)}, f32[1,896]{1,0:T(1,128)}, f32[1,256]{1,0:T(1,128)}, bf16[4096,896]{1,0:T(8,128)(2,1)}, /*index=5*/bf16[896,4096]{1,0:T(8,128)(2,1)}) custom-call(bf16[4096,896]{1,0:T(8,128)(2,1)} %get-tuple-element.34.h_hbm, bf16[896,4096]{1,0:T(8,128)(2,1)} %get-tuple-element.35.ht_hbm, ...), custom_call_target="tpu_custom_call" | custom-call | tf_op jit(solution)/shard_map/upper/pallas_call | solution.py:325
  392.2 188.8 %lower.1 = (f32[19,32,896]{2,1,0:T(8,128)}, f32[19,112,256]{2,1,0:T(8,128)}, f32[1,896]{1,0:T(1,128)}, f32[1,256]{1,0:T(1,128)}, f32[8,128]{1,0:T(8,128)}) custom-call(f32[1,896]{1,0:T(1,128)} %get-tuple-element.37.sqd_in, f32[1,256]{1,0:T(1,128)} %get-tuple-element.38.squ_in, bf16[4096,896]{1,0:T(8,128)(2,1)} %get-tuple-element.39.dh_hbm, ...), custom_call_target="tpu_custom_call" | custom-call | tf_op jit(solution)/shard_map/lower/pallas_call | solution.py:418
  581.6 13.9 %adam_down.1 = (bf16[2,608,896]{2,1,0:T(8,128)(2,1)}, f32[2,608,896]{2,1,0:T(8,128)}, f32[2,608,896]{2,1,0:T(8,128)}, f32[2,608,896]{2,1,0:T(8,128)}, f32[8,128]{1,0:T(8,128)}) custom-call(f32[8,128]{1,0:T(8,128)} %get-tuple-element.43.sq_ref, f32[1,1]{1,0:T(1,128)} %bitcast.8.clip_ref, f32[608,896]{1,0:T(8,128)} %bitcast.16, f32[608,896]{1,0:T(8,128)} %bitcast.15, ...), custom_call_target="tpu_custom_call" | custom-call | tf_op jit(solution)/shard_map/adam_down/pallas_call | solution.py:516
  595.5 18.0 %adam_up.1 = (bf16[2,112,4864]{2,1,0:T(8,128)(2,1)}, f32[2,112,4864]{2,1,0:T(8,128)}, f32[2,112,4864]{2,1,0:T(8,128)}, f32[2,112,4864]{2,1,0:T(8,128)}) custom-call(f32[8,128]{1,0:T(8,128)} %get-tuple-element.43.sq_ref, f32[1,1]{1,0:T(1,128)} %bitcast.7.clip_ref, f32[19,112,256]{2,1,0:T(8,128)} %get-tuple-element.44.one_ref, ...), custom_call_target="tpu_custom_call" | custom-call | tf_op jit(solution)/shard_map/adam_up/pallas_call | solution.py:516
  613.5 106.3 %gather.1 = (bf16[2,896,4864]{2,1,0:T(8,128)(2,1)}, bf16[2,4864,896]{2,1,0:T(8,128)(2,1)}) custom-call(bf16[2,112,4864]{2,1,0:T(8,128)(2,1)} %get-tuple-element.46.up_hbm, bf16[2,608,896]{2,1,0:T(8,128)(2,1)} %get-tuple-element.49.down_hbm), custom_call_target="tpu_custom_call" | custom-call | tf_op jit(solution)/shard_map/gather/pallas_call | solution.py:615
  719.8 1.2 slice.3
  721.0 0.0 copy-start
  721.0 15.0 %copy.23 = bf16[2,896,4864]{2,1,0:T(8,128)(2,1)} copy(bf16[2,896,4864]{2,1,0:T(8,128)(2,1)} %get-tuple-element.68) | data formatting | bytes 34865152
  736.0 2.5 copy-done
  738.5 6.4 copy.24
Async XLA Ops:
  721.0 17.5 %copy-start = (bf16[2,4864,896]{2,1,0:T(8,128)(2,1)S(1)}, bf16[2,4864,896]{2,1,0:T(8,128)(2,1)}, u32[]{:S(2)}) copy-start(bf16[2,4864,896]{2,1,0:T(8,128)(2,1)} %get-tuple-element.69) | copy-start | bytes 52297732

commit v4 on v3

v4 whole, which is shorter than its diff:
```python
import functools

import jax
import jax.numpy as jnp
from jax import lax
from jax.experimental import pallas as pl
from jax.experimental.pallas import tpu as pltpu
from jax.sharding import PartitionSpec as P

BETA1 = 0.9
BETA2 = 0.95
ADAM_EPS = 1e-8
LEARN_RATE = 5e-3
NORM_EPS = 1e-6
STEP = 10
BIAS_ONE = 1.0 - BETA1 ** STEP
BIAS_TWO = 1.0 - BETA2 ** STEP

F32 = jnp.float32
BF16 = jnp.bfloat16
ROWS = 4096
D = 896
FF = 4864
TILE = 256
NT = FF // TILE
OWN = 8
PIECE = TILE // OWN
UP_ROWS = D // OWN
DOWN_ROWS = FF // OWN
DEVICES = 16
RM = 256
NB = ROWS // RM
VMEM_LIMIT = 67_043_328


def gelu_value(pre_act):
    return pre_act * (0.5 + 0.5 * lax.erf(pre_act * 0.7071067811865476))


def gelu_both(pre_act):
    scaled = pre_act * 0.7071067811865476
    cdf = 0.5 + 0.5 * lax.erf(scaled)
    return pre_act * cdf, cdf + pre_act * jnp.exp2(scaled * scaled * -1.4426950408889634) * 0.3989422804014327


def mm(left, right):
    return jnp.dot(left, right, preferred_element_type=F32)


def mm_nt(left, right):
    return lax.dot_general(left, right, (((1,), (1,)), ((), ())), preferred_element_type=F32)


MESH = pl.DeviceIdType.MESH
LAG = 4
TILES = 2 * NT
GRID = TILES + LAG
EARLY = 6


def coordinates():
    d = lax.axis_index('data')
    z = lax.axis_index('replica')
    c = lax.rem(d, 2)
    x = lax.rem(lax.div(d, 2), 2)
    y = lax.div(d, 4)
    peers = {
        'c': {'data': d + 1 - 2 * c},
        'x': {'data': d + 2 - 4 * x},
        'y': {'data': d + 4 - 8 * y},
        'z': {'replica': 1 - z},
    }
    return d, c, x, y, z, peers


def neighbour_barrier(peers):
    barrier = pltpu.get_barrier_semaphore()
    for peer in peers:
        pl.semaphore_signal(barrier, inc=1, device_id=peer, device_id_type=MESH)
    pl.semaphore_wait(barrier, len(peers))


def grad_scratch(rows, cols):
    return [pltpu.VMEM((2, 2, 2, rows, cols), F32),
            pltpu.VMEM((2, 2, 2, rows, cols), F32),
            pltpu.VMEM((2, 2, rows, cols), F32),
            pltpu.VMEM((2, 2, rows, cols), F32),
            pltpu.VMEM((2, rows, cols), F32),
            pltpu.VMEM((2, rows, cols), F32),
            pltpu.VMEM((rows, cols), F32),
            pltpu.VMEM((2, rows, cols), F32),
            pltpu.SemaphoreType.DMA((4, 2)),
            pltpu.SemaphoreType.DMA((4, 2))]


class Reducer:
    def __init__(self, scratch, x_first, t):
        (self.tile, self.in_core, self.chip, self.in_one, self.two, self.in_two, self.four, self.in_rep,
         self.send, self.recv) = scratch
        self.x_first = x_first
        self.t = t
        _, self.c, self.x, self.y, _, self.peers = coordinates()

    def copy(self, stage, tile_index):
        slot = lax.rem(tile_index + 2, 2)
        first, second = ('x', 'y') if self.x_first else ('y', 'x')
        if stage == 0:
            src, dst, peer = self.tile.at[:, :, 1 - self.c], self.in_core.at[slot], 'c'
        elif stage == 1:
            src = self.chip.at[:, 1 - self.x] if self.x_first else self.chip.at[1 - self.y]
            dst, peer = self.in_one.at[slot], first
        elif stage == 2:
            src = self.two.at[1 - self.y] if self.x_first else self.two.at[1 - self.x]
            dst, peer = self.in_two.at[slot], second
        else:
            src, dst, peer = self.four, self.in_rep.at[slot], 'z'
        return pltpu.make_async_remote_copy(
            src_ref=src, dst_ref=dst, send_sem=self.send.at[stage, slot], recv_sem=self.recv.at[stage, slot],
            device_id=self.peers[peer], device_id_type=MESH)

    def start(self):
        self.copy(0, self.t).start()

    def progress(self, out_ref, sq_ref):
        t = self.t

        @pl.when(t >= 4)
        def _():
            self.copy(3, t - 4).wait()
            total = self.four[...] + self.in_rep[lax.rem(t, 2)]
            out_ref[0] = total
            sq_ref[...] += jnp.sum((total * total).reshape(-1, 8, total.shape[1]), axis=0)

        @pl.when((t >= 3) & (t < TILES + 3))
        def _():
            self.copy(2, t - 3).wait()
            mine = self.two[self.y] if self.x_first else self.two[self.x]
            self.four[...] = mine + self.in_two[lax.rem(t + 1, 2)]
            self.copy(3, t - 3).start()

        @pl.when((t >= 2) & (t < TILES + 2))
        def _():
            self.copy(1, t - 2).wait()
            mine = self.chip[:, self.x] if self.x_first else self.chip[self.y]
            self.two[...] = mine + self.in_one[lax.rem(t, 2)]
            self.copy(2, t - 2).start()

        @pl.when((t >= 1) & (t < TILES + 1))
        def _():
            self.copy(0, t - 1).wait()
            self.chip[...] = self.tile[:, :, self.c] + self.in_core[lax.rem(t + 1, 2)]
            self.copy(1, t - 1).start()


def permuted(w_ref, out_ref):
    for t in range(NT):
        out_ref[:, t * TILE:(t + 1) * TILE] = jnp.concatenate(
            [w_ref[0, :, d * DOWN_ROWS + t * PIECE:d * DOWN_ROWS + (t + 1) * PIECE] for d in range(OWN)], axis=1)


PERM_ROWS = 64


def permute_first(w_up):
    return pl.pallas_call(
        permuted,
        grid=(D // PERM_ROWS,),
        in_specs=[pl.BlockSpec((1, PERM_ROWS, FF), lambda i: (0, i, 0))],
        out_specs=pl.BlockSpec((PERM_ROWS, FF), lambda i: (i, 0)),
        out_shape=jax.ShapeDtypeStruct((D, FF), w_up.dtype),
        name="permute_first",
    )(w_up)


def forward_kernel(x_ref, dy_ref, wu_ref, wd_ref, next_ref, z_ref, h_ref, ht_ref, xt_ref, dyt_ref, next_out, acc):
    t = pl.program_id(0)
    block = jnp.minimum(t, ROWS // TILE - 1)

    @pl.when(t == 0)
    def _():
        acc[...] = jnp.zeros_like(acc)

    wd = wd_ref[0, :, 0].reshape(TILE, D)
    permuted(next_ref, next_out)
    for r in range(NB + 1):
        if r < NB:
            rows = pl.ds(r * RM, RM)
            z_ref[0, rows, :] = mm(x_ref[rows, :], wu_ref[...]).astype(BF16)
        if r > 0:
            rows = pl.ds((r - 1) * RM, RM)
            u = gelu_value(z_ref[0, rows, :].astype(F32)).astype(BF16)
            acc[rows, :] += mm(u, wd)
        if r == 2:
            xt_ref[...] = x_ref[pl.ds(pl.multiple_of(block * TILE, TILE), TILE), :].T
        if r == 5:
            dyt_ref[...] = dy_ref[...].T

    @pl.when(t == NT - 1)
    def _():
        h_ref[...] = acc[...].astype(BF16)
        ht_ref[...] = h_ref[...].T


def forward(x, dy, w_one, w_down5, w_up):
    last = ROWS // TILE - 1
    last_perm = D // PERM_ROWS - 1
    once = pl.Buffered(1)
    return pl.pallas_call(
        forward_kernel,
        grid=(NT,),
        in_specs=[
            pl.BlockSpec((ROWS, D), lambda t: (0, 0), pipeline_mode=once),
            pl.BlockSpec((TILE, D), lambda t: (jnp.minimum(t, last), 0)),
            pl.BlockSpec((D, TILE), lambda t: (0, t)),
            pl.BlockSpec((1, OWN, 1, PIECE, D), lambda t: (0, 0, t, 0, 0)),
            pl.BlockSpec((1, PERM_ROWS, FF), lambda t: (1, jnp.minimum(t, last_perm), 0)),
        ],
        out_specs=[
            pl.BlockSpec((1, ROWS, TILE), lambda t: (t, 0, 0)),
            pl.BlockSpec((ROWS, D), lambda t: (0, 0), pipeline_mode=once),
            pl.BlockSpec((D, ROWS), lambda t: (0, 0), pipeline_mode=once),
            pl.BlockSpec((D, TILE), lambda t: (0, jnp.minimum(t, last))),
            pl.BlockSpec((D, TILE), lambda t: (0, jnp.minimum(t, last))),
            pl.BlockSpec((PERM_ROWS, FF), lambda t: (jnp.minimum(t, last_perm), 0)),
        ],
        out_shape=[jax.ShapeDtypeStruct((NT, ROWS, TILE), BF16), jax.ShapeDtypeStruct((ROWS, D), BF16),
                   jax.ShapeDtypeStruct((D, ROWS), BF16), jax.ShapeDtypeStruct((D, ROWS), BF16),
                   jax.ShapeDtypeStruct((D, ROWS), BF16), jax.ShapeDtypeStruct((D, FF), BF16)],
        scratch_shapes=[pltpu.VMEM((ROWS, D), F32)],
        compiler_params=pltpu.CompilerParams(vmem_limit_bytes=VMEM_LIMIT),
        name="forward",
    )(x, dy, w_one, w_down5, w_up)


def backward_kernel(h_hbm, ht_hbm, dy_hbm, dyt_hbm, xt_hbm, wu_ref, wd_ref, z_ref, gd_ref, gu_ref, norm_ref,
                    h, ht, dy, dyt, acc, u_s, d_s, part_down, part_up, sq_down, sq_up, sems,
                    sq_mine, sq_all, sq_send, sq_recv, *grads):
    t = pl.program_id(0)
    loads = [pltpu.make_async_copy(s, v, sems.at[i]) for i, (s, v) in
             enumerate([(h_hbm, h), (dy_hbm, dy), (dyt_hbm, dyt), (ht_hbm, ht), (xt_hbm, ht)])]
    down = Reducer(grads[:10], True, t)
    up = Reducer(grads[10:], False, t)
    me = lax.axis_index('data')
    others = [{'data': lax.rem(me + k, OWN)} for k in range(1, OWN)]
    upper = t < NT
    lower = (t >= NT) & (t < TILES)

    @pl.when(t == 0)
    def _():
        for copy in loads[:4]:
            copy.start()
        neighbour_barrier(others + [down.peers['z']])
        acc[...] = jnp.zeros_like(acc)
        sq_down[...] = jnp.zeros_like(sq_down)
        sq_up[...] = jnp.zeros_like(sq_up)
        loads[0].wait()
        loads[1].wait()

    def upper_rows(first, last):
        wu = wu_ref[...]
        wd = wd_ref[0, :, 0].reshape(TILE, D)
        for r in range(first, last):
            if r < NB:
                rows = pl.ds(r * RM, RM)
                u_s[rows, :] = mm(h[rows, :], wu).astype(BF16)
                d_s[rows, :] = mm_nt(dy[rows, :], wd).astype(BF16)
            if r > 0:
                rows = pl.ds((r - 1) * RM, RM)
                u, slope = gelu_both(u_s[rows, :].astype(F32))
                dz = (d_s[rows, :].astype(F32) * slope).astype(BF16)
                u_s[rows, :] = u.astype(BF16)
                d_s[rows, :] = dz
                acc[rows, :] += mm_nt(dz, wu)

    def lower_rows(first, last):
        wd = wd_ref[0, :, 0].reshape(TILE, D)
        for r in range(first, last):
            if r < NB:
                rows = pl.ds(r * RM, RM)
                d_s[rows, :] = mm_nt(h[rows, :], wd).astype(BF16)
            if r > 0:
                rows = pl.ds((r - 1) * RM, RM)
                u, slope = gelu_both(z_ref[0, rows, :].astype(F32))
                u_s[rows, :] = u.astype(BF16)
                d_s[rows, :] = (d_s[rows, :].astype(F32) * slope).astype(BF16)

    def grads_early(rows):
        part_down[...] = mm(dyt[:, :rows], u_s[:rows, :])
        part_up[...] = mm(ht[:, :rows], d_s[:rows, :])

    def grads_late(rows):
        down.tile[...] = (part_down[...] + mm(dyt[:, rows:], u_s[rows:, :])).T.reshape(2, 2, 2, PIECE, D)
        up.tile[...] = (part_up[...] + mm(ht[:, rows:], d_s[rows:, :])).reshape(2, 2, 2, UP_ROWS, TILE)

    early = EARLY * RM

    @pl.when(upper)
    def _():
        upper_rows(0, EARLY + 1)

    @pl.when(lower)
    def _():
        lower_rows(0, EARLY + 1)

    down.progress(gd_ref, sq_down)

    @pl.when(t == 0)
    def _():
        loads[2].wait()
        loads[3].wait()

    @pl.when(t == NT)
    def _():
        loads[4].wait()

    @pl.when(upper)
    def _():
        upper_rows(EARLY + 1, NB)
        grads_early(early)

    @pl.when(lower)
    def _():
        lower_rows(EARLY + 1, NB)
        grads_early(early)

    up.progress(gu_ref, sq_up)

    @pl.when(upper)
    def _():
        upper_rows(NB, NB + 1)
        grads_late(early)

    @pl.when(lower)
    def _():
        lower_rows(NB, NB + 1)
        grads_late(early)

    @pl.when(t < TILES)
    def _():
        down.start()
        up.start()

    @pl.when(t == NT - 1)
    def _():
        loads[4].start()
        h[...] = acc[...].astype(BF16)
        dyt[...] = h[...].T

    @pl.when(t == GRID - 1)
    def _():
        part = jnp.sum(sq_down[...], axis=1, keepdims=True) + jnp.sum(sq_up[...], axis=1, keepdims=True)
        part = jnp.sum(part, axis=0, keepdims=True)
        sq_mine[...] = jnp.broadcast_to(part, sq_mine.shape)
        sq_all[me] = sq_mine[...]
        copies = [pltpu.make_async_remote_copy(
            src_ref=sq_mine, dst_ref=sq_all.at[me], send_sem=sq_send.at[k], recv_sem=sq_recv.at[k],
            device_id=others[k], device_id_type=MESH) for k in range(OWN - 1)]
        for copy in copies:
            copy.start()
        for copy in copies:
            copy.wait()
        total = sq_all[0]
        for k in range(1, OWN):
            total = total + sq_all[k]
        norm_ref[...] = total


def backward(h, ht, dy, dyt, xt, w_two, w_down5, z):
    anyspec = pl.BlockSpec(memory_space=pl.ANY)

    def final_tile(t):
        return jnp.clip(t - LAG, 0, TILES - 1)

    def layer_and_tile(t):
        first = t < NT
        return jnp.where(first, 1, 0), jnp.where(first, t, jnp.minimum(t - NT, NT - 1))

    def down_index(t):
        layer, tile = layer_and_tile(t)
        return layer, 0, tile, 0, 0

    return pl.pallas_call(
        backward_kernel,
        grid=(GRID,),
        in_specs=[anyspec] * 5 + [
            pl.BlockSpec((D, TILE), lambda t: (0, jnp.minimum(t, NT - 1))),
            pl.BlockSpec((1, OWN, 1, PIECE, D), down_index),
            pl.BlockSpec((1, ROWS, TILE), lambda t: (jnp.clip(t - NT, 0, NT - 1), 0, 0)),
        ],
        out_specs=[
            pl.BlockSpec((1, PIECE, D), lambda t: (final_tile(t), 0, 0)),
            pl.BlockSpec((1, UP_ROWS, TILE), lambda t: (final_tile(t), 0, 0)),
            pl.BlockSpec((8, 128), lambda t: (0, 0)),
        ],
        out_shape=[jax.ShapeDtypeStruct((TILES, PIECE, D), F32), jax.ShapeDtypeStruct((TILES, UP_ROWS, TILE), F32),
                   jax.ShapeDtypeStruct((8, 128), F32)],
        scratch_shapes=[pltpu.VMEM((ROWS, D), BF16), pltpu.VMEM((D, ROWS), BF16),
                        pltpu.VMEM((ROWS, D), BF16), pltpu.VMEM((D, ROWS), BF16),
                        pltpu.VMEM((ROWS, D), F32), pltpu.VMEM((ROWS, TILE), BF16), pltpu.VMEM((ROWS, TILE), BF16),
                        pltpu.VMEM((D, TILE), F32), pltpu.VMEM((D, TILE), F32),
                        pltpu.VMEM((8, D), F32), pltpu.VMEM((8, TILE), F32),
                        pltpu.SemaphoreType.DMA((5,)),
                        pltpu.VMEM((8, 128), F32), pltpu.VMEM((OWN, 8, 128), F32),
                        pltpu.SemaphoreType.DMA((OWN - 1,)), pltpu.SemaphoreType.DMA((OWN - 1,))]
        + grad_scratch(PIECE, D) + grad_scratch(UP_ROWS, TILE),
        compiler_params=pltpu.CompilerParams(vmem_limit_bytes=VMEM_LIMIT, collective_id=0, has_side_effects=True),
        name="backward",
    )(h, ht, dy, dyt, xt, w_two, w_down5, z)


def adam_update(grad_vals, master_vals, mom_vals, var_vals, clip_scale):
    new_mom = BETA1 * mom_vals + (1.0 - BETA1) * clip_scale * grad_vals
    new_var = BETA2 * var_vals + (1.0 - BETA2) * (clip_scale * clip_scale) * (grad_vals * grad_vals)
    new_master = master_vals - LEARN_RATE * (new_mom / BIAS_ONE) / (jnp.sqrt(new_var / BIAS_TWO) + ADAM_EPS)
    return new_master, new_mom, new_var


def norm_and_clip(sq_ref, clip_ref):
    norm = jnp.sqrt(sq_ref[...]) / DEVICES
    return norm, jnp.minimum(1.0, clip_ref[0, 0] / (norm + NORM_EPS))[0:1, 0:1]


def adam_up_kernel(sq_ref, clip_ref, g_ref, master_ref, mom_ref, var_ref,
                   new_w_ref, new_master_ref, new_mom_ref, new_var_ref):
    _, scale = norm_and_clip(sq_ref, clip_ref)
    for n in range(FF // 128):
        pieces = [divmod(4 * n + q, NT) for q in range(4)]
        grad = jnp.concatenate([g_ref[t, :, d * PIECE:(d + 1) * PIECE] for d, t in pieces], axis=1) / DEVICES
        cols = pl.ds(n * 128, 128)
        master, mom, var = adam_update(grad, master_ref[0, :, cols], mom_ref[0, :, cols], var_ref[0, :, cols], scale)
        new_master_ref[0, :, cols] = master
        new_mom_ref[0, :, cols] = mom
        new_var_ref[0, :, cols] = var
        new_w_ref[0, :, cols] = master.astype(BF16)


def adam_down_kernel(sq_ref, clip_ref, g_ref, master_ref, mom_ref, var_ref,
                     new_w_ref, new_master_ref, new_mom_ref, new_var_ref, norm_ref):
    norm, scale = norm_and_clip(sq_ref, clip_ref)
    norm_ref[...] = norm

    def body(i, carry):
        rows = pl.ds(pl.multiple_of(i * 16, 16), 16)
        master, mom, var = adam_update(g_ref[0, rows, :] / DEVICES, master_ref[0, rows, :], mom_ref[0, rows, :],
                                       var_ref[0, rows, :], scale)
        new_master_ref[0, rows, :] = master
        new_mom_ref[0, rows, :] = mom
        new_var_ref[0, rows, :] = var
        new_w_ref[0, rows, :] = master.astype(BF16)
        return carry

    lax.fori_loop(0, g_ref.shape[1] // 16, body, 0)


def adam_call(kernel, name, square_sum, clip, grad, g_spec, master, mom, var, block, with_norm):
    layers, rows, cols = master.shape
    state = pl.BlockSpec((1, block, cols), lambda layer, i: (layer, i, 0))
    small = pl.BlockSpec((8, 128), lambda layer, i: (0, 0))
    out_specs = [state] * 4 + ([small] if with_norm else [])
    out_shape = [jax.ShapeDtypeStruct(master.shape, BF16)] + [jax.ShapeDtypeStruct(master.shape, F32)] * 3
    if with_norm:
        out_shape = out_shape + [jax.ShapeDtypeStruct((8, 128), F32)]
    return pl.pallas_call(
        kernel,
        grid=(layers, rows // block),
        in_specs=[small, pl.BlockSpec(memory_space=pltpu.SMEM), g_spec, state, state, state],
        out_specs=out_specs,
        out_shape=out_shape,
        compiler_params=pltpu.CompilerParams(vmem_limit_bytes=VMEM_LIMIT),
        name=name,
    )(square_sum, clip, grad, master, mom, var)


UP_CHUNKS = [(True, 0, 16), (True, 16, 32), (True, 48, 32), (True, 80, 32)]
DOWN_CHUNKS = [(False, 0, 144), (False, 144, 144), (False, 288, 160), (False, 448, 160)]
CHUNKS = UP_CHUNKS + DOWN_CHUNKS
NC = len(CHUNKS)
GROUPS = 14


def gather_kernel(up_hbm, down_hbm, out_up, out_down, up_v, down_v, send, recv, local):
    d, c, x, y, z, peers = coordinates()
    d_x = d + 2 - 4 * x
    d_y = d + 4 - 8 * y
    d_xy = d_x + 4 - 8 * y
    other_core = 1 - 2 * c

    loads = [pltpu.make_async_copy(up_hbm, up_v, local.at[0]), pltpu.make_async_copy(down_hbm, down_v, local.at[1])]
    for copy in loads:
        copy.start()
    neighbour_barrier([peers[k] for k in 'cxyz'])
    for copy in loads:
        copy.wait()

    def region(chunk, layer, owner):
        is_up, first, count = CHUNKS[chunk]
        out, rows = (out_up, UP_ROWS) if is_up else (out_down, DOWN_ROWS)
        return out.at[layer, pl.ds(pl.multiple_of(owner * rows + first, 16), count)]

    def mine(chunk, layer):
        is_up, first, count = CHUNKS[chunk]
        return (up_v if is_up else down_v).at[layer, pl.ds(first, count)]

    started = []

    def send_chunk(group, chunk, src, layer, owner, peer):
        copy = pltpu.make_async_remote_copy(
            src_ref=src, dst_ref=region(chunk, layer, owner), send_sem=send.at[group, chunk],
            recv_sem=recv.at[group, chunk], device_id=peers[peer], device_id_type=MESH)
        copy.start()
        started.append(copy)

    def arrived(group, chunk, layer, owner):
        pltpu.make_async_remote_copy(
            src_ref=region(chunk, layer, owner), dst_ref=region(chunk, layer, owner), send_sem=send.at[group, chunk],
            recv_sem=recv.at[group, chunk], device_id=peers['c'], device_id_type=MESH).wait_recv()

    for k in range(NC):
        send_chunk(0, k, mine(k, z), z, d, 'x')
        send_chunk(1, k, mine(k, 1 - z), 1 - z, d, 'y')
    for k in range(NC):
        send_chunk(6, k, mine(k, 0), 0, d, 'c')
        send_chunk(7, k, mine(k, 1), 1, d, 'c')
    stores = []
    for layer in range(2):
        stores.append(pltpu.make_async_copy(up_v.at[layer], out_up.at[layer, pl.ds(pl.multiple_of(d * UP_ROWS, 16), UP_ROWS)], local.at[2 + layer]))
        stores.append(pltpu.make_async_copy(down_v.at[layer], out_down.at[layer, pl.ds(pl.multiple_of(d * DOWN_ROWS, 16), DOWN_ROWS)], local.at[4 + layer]))
    for copy in stores:
        copy.start()

    def second(k):
        for group, core_group, layer, owner in ((4, 10, 1 - z, d_x), (5, 11, z, d_y), (2, 12, z, d_xy), (3, 13, 1 - z, d_xy)):
            arrived(group, k, layer, owner)
            send_chunk(core_group, k, region(k, layer, owner), layer, owner, 'c')

    for k in range(NC):
        arrived(0, k, z, d_x)
        src = region(k, z, d_x)
        send_chunk(4, k, src, z, d_x, 'z')
        send_chunk(2, k, src, z, d_x, 'y')
        send_chunk(8, k, src, z, d_x, 'c')
        arrived(1, k, 1 - z, d_y)
        src = region(k, 1 - z, d_y)
        send_chunk(5, k, src, 1 - z, d_y, 'z')
        send_chunk(3, k, src, 1 - z, d_y, 'x')
        send_chunk(9, k, src, 1 - z, d_y, 'c')
    for k in range(NC):
        second(k)
    for k in range(NC):
        for group, layer, owner in ((6, 0, d), (7, 1, d), (8, z, d_x), (9, 1 - z, d_y), (10, 1 - z, d_x),
                                    (11, z, d_y), (12, z, d_xy), (13, 1 - z, d_xy)):
            arrived(group, k, layer, owner + other_core)
    for copy in started:
        copy.wait_send()
    for copy in stores:
        copy.wait()


def gather(up_shard, down_shard):
    anyspec = pl.BlockSpec(memory_space=pl.ANY)
    return pl.pallas_call(
        gather_kernel,
        in_specs=[anyspec, anyspec],
        out_specs=[anyspec, anyspec],
        out_shape=[jax.ShapeDtypeStruct((2, D, FF), BF16), jax.ShapeDtypeStruct((2, FF, D), BF16)],
        scratch_shapes=[pltpu.VMEM((2, UP_ROWS, FF), BF16), pltpu.VMEM((2, DOWN_ROWS, D), BF16),
                        pltpu.SemaphoreType.DMA((GROUPS, NC)), pltpu.SemaphoreType.DMA((GROUPS, NC)),
                        pltpu.SemaphoreType.DMA((6,))],
        compiler_params=pltpu.CompilerParams(vmem_limit_bytes=VMEM_LIMIT, collective_id=2, has_side_effects=True),
        name="gather",
    )(up_shard, down_shard)


def solution(mesh):
    batch_spec = P(('replica', 'data'), None)
    whole_spec = P()
    shard_spec = P(None, 'data', None)

    def device_step(inp_rows, out_grad, w_up, w_down, master_up, master_down, mom_up, mom_down, var_up, var_down, clip_norm):
        w_one = permute_first(w_up)
        w_down5 = w_down.reshape(2, OWN, NT, PIECE, D)
        pre_one, mid_rows, mid_t, inp_t, grad_t, w_two = forward(inp_rows, out_grad, w_one, w_down5, w_up)
        grad_down, grad_up, square_sum = backward(mid_rows, mid_t, out_grad, grad_t, inp_t, w_two, w_down5, pre_one)
        clip = clip_norm.reshape(1, 1)
        w_up_shard, master_up_new, mom_up_new, var_up_new = adam_call(
            adam_up_kernel, "adam_up", square_sum, clip, grad_up,
            pl.BlockSpec((NT, 16, TILE), lambda layer, i: (1 - layer, i, 0)), master_up, mom_up, var_up, 16, False)
        w_down_shard, master_down_new, mom_down_new, var_down_new, norm = adam_call(
            adam_down_kernel, "adam_down", square_sum, clip, grad_down.reshape(2, DOWN_ROWS, D),
            pl.BlockSpec((1, 304, D), lambda layer, i: (1 - layer, i, 0)), master_down, mom_down, var_down, 304, True)
        w_up_new, w_down_new = gather(w_up_shard, w_down_shard)
        return (w_up_new, w_down_new, master_up_new, master_down_new, mom_up_new, mom_down_new, var_up_new, var_down_new, norm[0, 0])

    return jax.shard_map(device_step, mesh=mesh, in_specs=(batch_spec, batch_spec, whole_spec, whole_spec, shard_spec, shard_spec, shard_spec, shard_spec, shard_spec, shard_spec, whole_spec), out_specs=(whole_spec, whole_spec, shard_spec, shard_spec, shard_spec, shard_spec, shard_spec, shard_spec, whole_spec), check_vma=False)
```

time: 746 us -> 714 us (0.957)
  Pallas kernels: 719 us -> 687 us
    pallas_call x5 -> x4, Pallas kernels: 511 us -> 475 us  [the longest x1 429 us: backward(): pl.pallas_call(backward_kernel, grid=(GRID,), in_specs=[anyspec] * 5 + [p...]
where the time goes in v4:
time: 714 us; the launch traced here: 713 us
  Pallas kernels  687 us (96%)
  local copies, waits for them, and re-layouts  25.1 us (4%)
    pallas_call x1, Pallas kernels, backward(): pl.pallas_call(backward_kernel, grid=(GRID,), in_specs=[anyspec] * 5 + [p...  429 us
    pallas_call x1, Pallas kernels, gather(): pl.pallas_call(gather_kernel, in_specs=[anyspec, anyspec], out_specs=[any...  106 us
    pallas_call x1, Pallas kernels, forward(): pl.pallas_call(forward_kernel, grid=(NT,), in_specs=[pl.BlockSpec((ROWS,...  106 us
    pallas_call x2, Pallas kernels, adam_call(): pl.pallas_call(kernel, grid=(layers, rows // block), in_specs=[small, pl....  31.7 us
    unnamed x4, local copies, waits for them, and re-layouts  23.9 us
    pallas_call x1, Pallas kernels, permute_first(): pl.pallas_call(permuted, grid=(D // PERM_ROWS,), in_specs=[pl.BlockSpec((...  14.4 us

profile of v4, /device:TPU:0, one launch (start us, length us, event | category | flops | bytes accessed | tf_op | source)
XLA Modules:
  0.0 713.0 jit_solution(18125342651756542007)
XLA Ops:
  0.6 14.4 %permute_first.1.wu_ref = bf16[896,4864]{1,0:T(8,128)(2,1)} custom-call(bf16[2,896,4864]{2,1,0:T(8,128)(2,1)} %next_ref.1), custom_call_target="tpu_custom_call" | custom-call | tf_op jit(solution)/shard_map/permute_first/pallas_call | solution.py:165
  15.1 106.0 %forward.1 = (bf16[19,4096,256]{2,1,0:T(8,128)(2,1)}, bf16[4096,896]{1,0:T(8,128)(2,1)}, bf16[896,4096]{1,0:T(8,128)(2,1)}, bf16[896,4096]{1,0:T(8,128)(2,1)}, b...) custom-call(bf16[4096,896]{1,0:T(8,128)(2,1)} %x_ref.1, bf16[4096,896]{1,0:T(8,128)(2,1)} %dy_hbm.1, ...), custom_call_target="tpu_custom_call" | custom-call | tf_op jit(solution)/shard_map/forward/pallas_call | solution.py:208
  121.0 428.6 %backward.1 = (f32[38,32,896]{2,1,0:T(8,128)}, f32[38,112,256]{2,1,0:T(8,128)}, f32[8,128]{1,0:T(8,128)}) custom-call(bf16[4096,896]{1,0:T(8,128)(2,1)} %get-tuple-element.29.h_hbm, bf16[896,4096]{1,0:T(8,128)(2,1)} %get-tuple-element.30.ht_hbm, bf16[4096,896]{1,0:T(8,128)(2,1)} %dy_hbm.1, bf16[896,4096]{1,0:T(8,128)(2,1)} %get-tuple-element.31.dyt_hbm, ...), custom_call_target="tpu_custom_call" | custom-call | tf_op jit(solution)/shard_map/backward/pallas_call | solution.py:382
  550.2 14.1 %adam_down.1 = (bf16[2,608,896]{2,1,0:T(8,128)(2,1)}, f32[2,608,896]{2,1,0:T(8,128)}, f32[2,608,896]{2,1,0:T(8,128)}, f32[2,608,896]{2,1,0:T(8,128)}, f32[8,128]{1,0:T(8,128)}) custom-call(f32[8,128]{1,0:T(8,128)} %get-tuple-element.35.sq_ref, f32[1,1]{1,0:T(1,128)} %bitcast.5.clip_ref, f32[2,608,896]{2,1,0:T(8,128)} %bitcast.8, f32[2,608,896]{2,1,0:T(8,128)} %master_ref.3, ...), custom_call_target="tpu_custom_call" | custom-call | tf_op jit(solution)/shard_map/adam_down/pallas_call | solution.py:463
  564.4 17.5 %adam_up.1 = (bf16[2,112,4864]{2,1,0:T(8,128)(2,1)}, f32[2,112,4864]{2,1,0:T(8,128)}, f32[2,112,4864]{2,1,0:T(8,128)}, f32[2,112,4864]{2,1,0:T(8,128)}) custom-call(f32[8,128]{1,0:T(8,128)} %get-tuple-element.35.sq_ref, f32[1,1]{1,0:T(1,128)} %bitcast.4.clip_ref, f32[38,112,256]{2,1,0:T(8,128)} %get-tuple-element.36.g_ref, f32[2,112,4864]{2,1,0:T(8,128)} %master_ref.2, ...), custom_call_target="tpu_custom_call" | custom-call | tf_op jit(solution)/shard_map/adam_up/pallas_call | solution.py:463
  581.9 106.1 %gather.1 = (bf16[2,896,4864]{2,1,0:T(8,128)(2,1)}, bf16[2,4864,896]{2,1,0:T(8,128)(2,1)}) custom-call(bf16[2,112,4864]{2,1,0:T(8,128)(2,1)} %get-tuple-element.37.up_hbm, bf16[2,608,896]{2,1,0:T(8,128)(2,1)} %get-tuple-element.39.down_hbm), custom_call_target="tpu_custom_call" | custom-call | tf_op jit(solution)/shard_map/gather/pallas_call | solution.py:561
  688.0 1.2 slice.3
  689.2 0.0 copy-start
  689.2 15.0 %copy.23 = bf16[2,896,4864]{2,1,0:T(8,128)(2,1)} copy(bf16[2,896,4864]{2,1,0:T(8,128)(2,1)} %get-tuple-element.58) | data formatting | bytes 34865152
  704.1 2.5 copy-done
  706.7 6.4 copy.24
Async XLA Ops:
  689.2 17.5 %copy-start = (bf16[2,4864,896]{2,1,0:T(8,128)(2,1)S(1)}, bf16[2,4864,896]{2,1,0:T(8,128)(2,1)}, u32[]{:S(2)}) copy-start(bf16[2,4864,896]{2,1,0:T(8,128)(2,1)} %get-tuple-element.59) | copy-start | bytes 52297732

commit v5 on v4

--- a/solution.py
+++ b/solution.py
@@ -55,7 +55,7 @@
 LAG = 4
 TILES = 2 * NT
 GRID = TILES + LAG
-EARLY = 6
+EARLY = 12
 
 
 def coordinates():
@@ -411,7 +411,7 @@
 def adam_update(grad_vals, master_vals, mom_vals, var_vals, clip_scale):
     new_mom = BETA1 * mom_vals + (1.0 - BETA1) * clip_scale * grad_vals
     new_var = BETA2 * var_vals + (1.0 - BETA2) * (clip_scale * clip_scale) * (grad_vals * grad_vals)
-    new_master = master_vals - LEARN_RATE * (new_mom / BIAS_ONE) / (jnp.sqrt(new_var / BIAS_TWO) + ADAM_EPS)
+    new_master = master_vals - (LEARN_RATE / BIAS_ONE) * new_mom / (jnp.sqrt(new_var * (1.0 / BIAS_TWO)) + ADAM_EPS)
     return new_master, new_mom, new_var
 
 
@@ -425,7 +425,7 @@
     _, scale = norm_and_clip(sq_ref, clip_ref)
     for n in range(FF // 128):
         pieces = [divmod(4 * n + q, NT) for q in range(4)]
-        grad = jnp.concatenate([g_ref[t, :, d * PIECE:(d + 1) * PIECE] for d, t in pieces], axis=1) / DEVICES
+        grad = jnp.concatenate([g_ref[t, :, d * PIECE:(d + 1) * PIECE] for d, t in pieces], axis=1) * (1.0 / DEVICES)
         cols = pl.ds(n * 128, 128)
         master, mom, var = adam_update(grad, master_ref[0, :, cols], mom_ref[0, :, cols], var_ref[0, :, cols], scale)
         new_master_ref[0, :, cols] = master
@@ -441,7 +441,7 @@
 
     def body(i, carry):
         rows = pl.ds(pl.multiple_of(i * 16, 16), 16)
-        master, mom, var = adam_update(g_ref[0, rows, :] / DEVICES, master_ref[0, rows, :], mom_ref[0, rows, :],
+        master, mom, var = adam_update(g_ref[0, rows, :] * (1.0 / DEVICES), master_ref[0, rows, :], mom_ref[0, rows, :],
                                        var_ref[0, rows, :], scale)
         new_master_ref[0, rows, :] = master
         new_mom_ref[0, rows, :] = mom

time: 714 us -> 713 us (level)
  no operation moved by 1% of the time
where the time goes in v5:
time: 713 us; the launch traced here: 712 us
  Pallas kernels  686 us (96%)
  local copies, waits for them, and re-layouts  25.1 us (4%)
    pallas_call x1, Pallas kernels, backward(): pl.pallas_call(backward_kernel, grid=(GRID,), in_specs=[anyspec] * 5 + [p...  427 us
    pallas_call x1, Pallas kernels, gather(): pl.pallas_call(gather_kernel, in_specs=[anyspec, anyspec], out_specs=[any...  106 us
    pallas_call x1, Pallas kernels, forward(): pl.pallas_call(forward_kernel, grid=(NT,), in_specs=[pl.BlockSpec((ROWS,...  106 us
    pallas_call x2, Pallas kernels, adam_call(): pl.pallas_call(kernel, grid=(layers, rows // block), in_specs=[small, pl....  31.6 us
    unnamed x4, local copies, waits for them, and re-layouts  23.9 us
    pallas_call x1, Pallas kernels, permute_first(): pl.pallas_call(permuted, grid=(D // PERM_ROWS,), in_specs=[pl.BlockSpec((...  14.4 us

profile of v5, /device:TPU:0, one launch (start us, length us, event | category | flops | bytes accessed | tf_op | source)
XLA Modules:
  0.0 712.1 jit_solution(18001675655191904022)
XLA Ops:
  0.6 14.4 %permute_first.1.wu_ref = bf16[896,4864]{1,0:T(8,128)(2,1)} custom-call(bf16[2,896,4864]{2,1,0:T(8,128)(2,1)} %next_ref.1), custom_call_target="tpu_custom_call" | custom-call | tf_op jit(solution)/shard_map/permute_first/pallas_call | solution.py:165
  15.1 106.0 %forward.1 = (bf16[19,4096,256]{2,1,0:T(8,128)(2,1)}, bf16[4096,896]{1,0:T(8,128)(2,1)}, bf16[896,4096]{1,0:T(8,128)(2,1)}, bf16[896,4096]{1,0:T(8,128)(2,1)}, b...) custom-call(bf16[4096,896]{1,0:T(8,128)(2,1)} %x_ref.1, bf16[4096,896]{1,0:T(8,128)(2,1)} %dy_hbm.1, ...), custom_call_target="tpu_custom_call" | custom-call | tf_op jit(solution)/shard_map/forward/pallas_call | solution.py:208
  121.0 427.5 %backward.1 = (f32[38,32,896]{2,1,0:T(8,128)}, f32[38,112,256]{2,1,0:T(8,128)}, f32[8,128]{1,0:T(8,128)}) custom-call(bf16[4096,896]{1,0:T(8,128)(2,1)} %get-tuple-element.29.h_hbm, bf16[896,4096]{1,0:T(8,128)(2,1)} %get-tuple-element.30.ht_hbm, bf16[4096,896]{1,0:T(8,128)(2,1)} %dy_hbm.1, bf16[896,4096]{1,0:T(8,128)(2,1)} %get-tuple-element.31.dyt_hbm, ...), custom_call_target="tpu_custom_call" | custom-call | tf_op jit(solution)/shard_map/backward/pallas_call | solution.py:382
  549.1 14.1 %adam_down.1 = (bf16[2,608,896]{2,1,0:T(8,128)(2,1)}, f32[2,608,896]{2,1,0:T(8,128)}, f32[2,608,896]{2,1,0:T(8,128)}, f32[2,608,896]{2,1,0:T(8,128)}, f32[8,128]{1,0:T(8,128)}) custom-call(f32[8,128]{1,0:T(8,128)} %get-tuple-element.35.sq_ref, f32[1,1]{1,0:T(1,128)} %bitcast.5.clip_ref, f32[2,608,896]{2,1,0:T(8,128)} %bitcast.8, f32[2,608,896]{2,1,0:T(8,128)} %master_ref.3, ...), custom_call_target="tpu_custom_call" | custom-call | tf_op jit(solution)/shard_map/adam_down/pallas_call | solution.py:463
  563.2 17.5 %adam_up.1 = (bf16[2,112,4864]{2,1,0:T(8,128)(2,1)}, f32[2,112,4864]{2,1,0:T(8,128)}, f32[2,112,4864]{2,1,0:T(8,128)}, f32[2,112,4864]{2,1,0:T(8,128)}) custom-call(f32[8,128]{1,0:T(8,128)} %get-tuple-element.35.sq_ref, f32[1,1]{1,0:T(1,128)} %bitcast.4.clip_ref, f32[38,112,256]{2,1,0:T(8,128)} %get-tuple-element.36.g_ref, f32[2,112,4864]{2,1,0:T(8,128)} %master_ref.2, ...), custom_call_target="tpu_custom_call" | custom-call | tf_op jit(solution)/shard_map/adam_up/pallas_call | solution.py:463
  580.7 106.3 %gather.1 = (bf16[2,896,4864]{2,1,0:T(8,128)(2,1)}, bf16[2,4864,896]{2,1,0:T(8,128)(2,1)}) custom-call(bf16[2,112,4864]{2,1,0:T(8,128)(2,1)} %get-tuple-element.37.up_hbm, bf16[2,608,896]{2,1,0:T(8,128)(2,1)} %get-tuple-element.39.down_hbm), custom_call_target="tpu_custom_call" | custom-call | tf_op jit(solution)/shard_map/gather/pallas_call | solution.py:561
  687.0 1.2 slice.3
  688.2 0.0 copy-start
  688.2 15.0 %copy.23 = bf16[2,896,4864]{2,1,0:T(8,128)(2,1)} copy(bf16[2,896,4864]{2,1,0:T(8,128)(2,1)} %get-tuple-element.58) | data formatting | bytes 34865152
  703.2 2.5 copy-done
  705.7 6.4 copy.24
Async XLA Ops:
  688.2 17.5 %copy-start = (bf16[2,4864,896]{2,1,0:T(8,128)(2,1)S(1)}, bf16[2,4864,896]{2,1,0:T(8,128)(2,1)}, u32[]{:S(2)}) copy-start(bf16[2,4864,896]{2,1,0:T(8,128)(2,1)} %get-tuple-element.59) | copy-start | bytes 52297732
